TPU v7x, 256 devices: a whole 4x4x8 slice. The times are simulated.
256 devices in a mesh: tok: 128 (over x, z, y), exp: 2 (over core).
Axes of the slice: x: 4, y: 4, z: 8, core: 2. Of those that a mesh axis runs over, the one named last changes fastest.
Arguments:
- activations: bfloat16 [3072, 14336], P(('tok', 'exp')), may hold values from -6 to 6
- expert_ids: int32 [3072, 2], P(('tok', 'exp')), may hold values from 0 to 7, all different within a row; in each aligned block of 12 rows (0 to 11, 12 to 23, ...) at most 4 rows name the same one
Outputs:
- hessian: float32 [2, 14336, 14336], P('exp', 'tok')
Inputs may be any that keep to these rules, and one draw needn't show every extreme that they name: `expert_ids`: each row names 2 different experts. Among the 12 rows of one device no expert is named more than 4 times, some expert exactly 4 times; every expert is named by some row.
All inputs are finite; a program needn't handle non-finite values.
Results may differ from a plain program's by a relative error of at most 0.0003.
Values may be sent and summed in bfloat16 or wider, within the bound.
A program may use at most 128 MiB of HBM per device.

v0:
```python
import math

import jax
import jax.numpy as jnp
from jax import lax
from jax.sharding import Mesh
from jax.sharding import PartitionSpec as P

CAP = 4
TOK = ("tok_0", "tok_1", "tok_2")
TOK_EXP = ("tok_0", "tok_1", "tok_2", "exp")


def side_by_side(arrays, axis, split_dim, concat_dim, along):
    widths = [math.prod(a.shape[along:]) for a in arrays]
    both = jnp.concatenate(
        [a.reshape(*a.shape[:along], w) for a, w in zip(arrays, widths)], axis=along
    )
    out = lax.all_to_all(both, axis, split_axis=split_dim, concat_axis=concat_dim, tiled=True)
    tiles = jnp.split(out, [sum(widths[:k]) for k in range(1, len(widths))], axis=along)
    return tuple((b.reshape(*out.shape[:along], *a.shape[along:]) for a, b in zip(arrays, tiles)))


def one_axis_at_a_time(value, axes):
    for axis in axes:
        value = lax.psum(value, axis)
    return value


def place_tokens(activations, expert_ids, window_size):
    expert_labels = jnp.arange(window_size, dtype=jnp.int32)
    routed = jnp.any(expert_ids[:, :, None] == expert_labels[None, None, :], axis=1).astype(
        jnp.int32
    )
    ranking = jnp.cumsum(routed, axis=0) - 1
    slot_labels = jnp.arange(CAP, dtype=jnp.int32)
    placement = (routed.T[:, None, :] == 1) & (ranking.T[:, None, :] == slot_labels[None, :, None])
    placement_b = placement.astype(jnp.bfloat16)
    send_slots = jnp.einsum(
        "gct,tf->gcf", placement_b, activations, preferred_element_type=jnp.float32
    ).astype(jnp.bfloat16)
    send_marks = jnp.sum(placement.astype(jnp.float32), axis=2).astype(jnp.bfloat16)
    return (send_slots, send_marks)


def shards(activations, expert_ids):
    window_size = lax.axis_size("exp")
    send_slots, send_marks = place_tokens(activations, expert_ids, window_size)
    owned, present = side_by_side((send_slots, send_marks), "exp", 0, 1, 2)
    received = owned[0]
    own_cols = lax.all_to_all(received, TOK, split_axis=1, concat_axis=0, tiled=True)
    routed_total = one_axis_at_a_time(jnp.sum(present.astype(jnp.float32)), TOK)
    product = lax.dot_general(
        own_cols,
        lax.all_gather(own_cols, TOK, axis=1, tiled=True),
        (((0,), (0,)), ((), ())),
        preferred_element_type=jnp.float32,
    )
    return (product * (2.0 / routed_total))[None]


def solution(mesh):
    split = Mesh(
        mesh.devices.reshape(4, 8, 4, mesh.shape["exp"]), ("tok_0", "tok_1", "tok_2", "exp")
    )
    return jax.shard_map(
        shards,
        mesh=split,
        in_specs=(P(TOK_EXP, None), P(TOK_EXP, None)),
        out_specs=P("exp", TOK, None),
        check_vma=False,
    )
```

profile of v0, /device:TPU:6, one launch (start us, length us, event | category | flops | bytes accessed | tf_op | source)
XLA Modules:
  0.0 254.6 jit_solution(10797280591592840811)
XLA Ops:
  6.5 0.0 copy-start
  6.5 0.0 all-gather.2.cloned.1.call-start
  6.5 0.7 compare_reduce_fusion
  7.3 0.2 reduce_window_sum.11
  7.5 0.1 convert_reduce_fusion.1
  7.6 0.1 copy.12
  7.7 0.0 copy-done
  7.7 0.2 convolution_convert_fusion
  7.9 0.1 pad_maximum_fusion
  8.0 3.9 %all_to_all.31 = bf16[2,4,14337]{2,1,0:T(4,128)(2,1)S(1)} all-to-all(bf16[2,4,14337]{2,1,0:T(4,128)(2,1)S(1)} %pad_maximum_fusion), channel_id=1, replica_groups=mesh['tok_0'=4,'tok_1'=8,'tok_2'=4,'exp'=2] {'exp'}, dimensions={0} | all-to-all | bytes 458784 | tf_op jit(solution)/shard_map/all_to_all | solution.py:19
  11.9 0.1 all_to_all.24
  12.1 0.4 all_to_all.25
  12.4 0.2 copy.13
  12.6 28.4 %all_to_all.32 = bf16[8,128,112]{2,0,1:T(8,128)(2,1)S(1)} all-to-all(bf16[8,128,112]{2,0,1:T(8,128)(2,1)S(1)} %copy.13), channel_id=1, replica_groups=mesh['tok_0'=4,'tok_1'=8,'tok_2'=4,'exp'=2] {'tok_0','tok_1','tok_2'}, dimensions={1} | all-to-all | bytes 458752 | tf_op jit(solution)/shard_map/all_to_all | solution.py:51
  40.9 0.8 copy.14
  41.8 0.0 all-gather.2.cloned.1.call-update
  41.8 0.7 convert_reduce_fusion
  42.5 9.8 %psum.21 = f32[]{:T(128)} all-reduce(f32[]{:T(128)} %convert_reduce_fusion), channel_id=1, replica_groups=mesh['tok_0'=4,'tok_1'=8,'tok_2'=4,'exp'=2] {'tok_0'}, use_global_device_ids=true, to_apply=%region_4.5 | all-reduce | flops 1 | bytes 8 | tf_op jit(solution)/shard_map/psum | solution.py:26
  52.2 16.1 %psum.22 = f32[]{:T(128)} all-reduce(f32[]{:T(128)} %psum.21), channel_id=1, replica_groups=mesh['tok_0'=4,'tok_1'=8,'tok_2'=4,'exp'=2] {'tok_1'}, use_global_device_ids=true, to_apply=%region_5.6 | all-reduce | flops 1 | bytes 8 | tf_op jit(solution)/shard_map/psum | solution.py:26
  68.4 9.4 %psum.23 = f32[]{:T(128)} all-reduce(f32[]{:T(128)} %psum.22), channel_id=1, replica_groups=mesh['tok_0'=4,'tok_1'=8,'tok_2'=4,'exp'=2] {'tok_2'}, use_global_device_ids=true, to_apply=%region_6.7 | all-reduce | flops 1 | bytes 8 | tf_op jit(solution)/shard_map/psum | solution.py:26
  78.4 152.4 %all-gather.2.cloned.1.call-done = bf16[1024,14336]{0,1:T(8,128)(2,1)} async-done(((bf16[1024,112]{0,1:T(8,128)(2,1)}), bf16[1024,14336]{0,1:T(8,128)(2,1)}) %all-gather.2.cloned.1.call-update) | async-done | bytes 29360144 | tf_op jit(solution)/shard_map/all_gather | solution.py:55
  230.8 16.9 %fusion = f32[1,112,14336]{2,1,0:T(8,128)} fusion(bf16[1024,14336]{0,1:T(8,128)(2,1)} %all-gather.2.cloned.1.call-done, f32[]{:T(128)S(6)} %div.3, bf16[8,128,112]{2,0,1:T(8,128)(2,1)S(1)} %all_to_all.32), kind=kOutput, calls=%fused_computation.1 | convolution fusion | flops 3289939968 | bytes 36012036 | tf_op jit(solution)/shard_map/dot_general | solution.py:53
  (3 shorter events, 0.0 us)
Async XLA Ops:
  6.5 1.2 copy-start
  6.5 224.3 %all-gather.2.cloned.1.call-start = ((), (), s32[]{:S(2)}) async-start(), calls=%async_computation.2 | async-start | bytes 29589504 | tf_op jit(solution)/shard_map/all_gather | solution.py:55
Sparse Core Ops, SparseCore 0:
  41.9 188.8 all-gather.1
where the time goes:
time: 255 us
  waiting for transfers between devices  152 us (60%)
  blocking collectives  67.5 us (26%)
  matrix products  17.1 us (7%)
  between operations  14.2 us (6%)
    all_gather x1, waiting for transfers between devices, shards(): lax.all_gather(own_cols, TOK, axis=1, tiled=True)  152 us
    psum x3, blocking collectives, one_axis_at_a_time(): value = lax.psum(value, axis)  35.3 us
    all_to_all x1, blocking collectives, shards(): lax.all_to_all(received, TOK, split_axis=1, concat_axis=0, tiled=True)  28.4 us
    dot_general x1, matrix products, shards(): lax.dot_general(own_cols, lax.all_gather(own_cols, TOK, axis=1, tiled=Tru...  16.9 us
  transfers between devices with their start and end apart: 1, of which 1 were waited for; matrix products, arithmetic and copies ran while one was open for 0% of the time, Pallas kernels for 0%

commit v1 on v0

v1 whole, which is shorter than its diff:
```python
import jax
import jax.numpy as jnp
from jax import lax
from jax.sharding import Mesh
from jax.sharding import PartitionSpec as P

CAP = 4
LANES = 128
RING = "tok_2"
PLANE = ("tok_0", "tok_1")
TOK = ("tok_0", "tok_1", "tok_2")
TOK_EXP = ("tok_0", "tok_1", "tok_2", "exp")


def place_tokens(activations, expert_ids, window_size):
    expert_labels = jnp.arange(window_size, dtype=jnp.int32)
    routed = jnp.any(expert_ids[:, :, None] == expert_labels[None, None, :], axis=1).astype(
        jnp.int32
    )
    ranking = jnp.cumsum(routed, axis=0) - 1
    slot_labels = jnp.arange(CAP, dtype=jnp.int32)
    placement = (routed.T[:, None, :] == 1) & (ranking.T[:, None, :] == slot_labels[None, :, None])
    placement_b = placement.astype(jnp.bfloat16)
    send_slots = jnp.einsum(
        "gct,tf->gcf", placement_b, activations, preferred_element_type=jnp.float32
    ).astype(jnp.bfloat16)
    return send_slots, jnp.sum(routed, axis=0)


def shards(activations, expert_ids):
    experts = lax.axis_size("exp")
    ring = lax.axis_size(RING)
    ff = activations.shape[1]
    tiles = ff // (ring * LANES)
    slots, counts = place_tokens(activations, expert_ids, experts)
    slots = slots.reshape(experts, CAP, tiles, ring, LANES).transpose(3, 0, 1, 2, 4)
    slots = slots.reshape(ring * experts, CAP, tiles * LANES)
    own = lax.all_to_all(slots, (RING, "exp"), split_axis=0, concat_axis=0, tiled=True)
    own = own.reshape(ring * experts * CAP, tiles * LANES)
    total = counts.astype(jnp.float32)
    for axis in TOK_EXP:
        total = lax.psum(total, axis)
    routed_total = total[lax.axis_index("exp")]

    cols = lax.all_gather(own, PLANE, axis=0, tiled=True)
    group = lax.axis_index("tok_0") * lax.axis_size("tok_1") + lax.axis_index("tok_1")
    rows = ff // lax.axis_size(PLANE)
    first = (group * rows) // LANES
    y = lax.axis_index(RING)
    mine = (first - y + ring - 1) // ring
    left = lax.dynamic_slice_in_dim(cols, mine * LANES, LANES, axis=1)
    left = lax.all_gather(left, RING, axis=0)
    order = (first + jnp.arange(ring)) % ring
    left = jnp.take(left, order, axis=0).transpose(1, 0, 2).reshape(cols.shape[0], ring * LANES)
    left = lax.dynamic_slice_in_dim(left, group * rows - first * LANES, rows, axis=1)
    product = lax.dot_general(
        left, cols, (((0,), (0,)), ((), ())), preferred_element_type=jnp.float32
    )
    out = lax.all_to_all(
        product.reshape(ring, rows // ring, tiles * LANES), RING, split_axis=0, concat_axis=0, tiled=True
    )
    out = out * (2.0 / routed_total)
    out = out.reshape(ring, rows // ring, tiles, LANES).transpose(1, 2, 0, 3)
    return out.reshape(1, rows // ring, ff)


def solution(mesh):
    split = Mesh(
        mesh.devices.reshape(4, 8, 4, mesh.shape["exp"]), ("tok_0", "tok_1", "tok_2", "exp")
    )
    return jax.shard_map(
        shards,
        mesh=split,
        in_specs=(P(TOK_EXP, None), P(TOK_EXP, None)),
        out_specs=P("exp", TOK, None),
        check_vma=False,
    )
```

time: 255 us -> 276 us (1.082)
  waiting for transfers between devices: 152 us -> 118 us
  local copies, waits for them, and re-layouts: 1.58 us -> 34.2 us
  blocking collectives: 67.5 us -> 87.1 us
  matrix products: 17.1 us -> 8.67 us
  other arithmetic: 1.82 us -> 7.27 us
  starting transfers between devices: 0.01 us -> 5.32 us
    psum x3 -> x4, blocking collectives: 35.3 us -> 75.6 us  [shards(): total = lax.psum(total, axis)]
    all_gather x1 -> x2, waiting for transfers between devices: 152 us -> 118 us  [the longest x1 91.9 us: shards(): cols = lax.all_gather(own, PLANE, axis=0, tiled=True)]
    all_to_all x2 -> x1, blocking collectives: 32.3 us -> 11.4 us  [shards(): lax.all_to_all(slots, (RING, 'exp'), split_axis=0, concat_axis=0, tiled=T...]
    reshape x0 -> x7, local copies, waits for them, and re-layouts: none -> 17.3 us  [the longest x1 8.18 us: shards(): return out.reshape(1, rows // ring, ff)]
    transpose x0 -> x1, local copies, waits for them, and re-layouts: none -> 12.1 us  [shards(): out = out.reshape(ring, rows // ring, tiles, LANES).transpose(1, 2, 0, 3)]
    dot_general x1, matrix products: 16.9 us -> 8.46 us  [shards(): lax.dot_general(left, cols, (((0,), (0,)), ((), ())), preferred_element_t...]
    mul x0 -> x1, other arithmetic: none -> 6 us  [shards(): out = out * (2.0 / routed_total)]
    all_to_all x0 -> x1, starting transfers between devices: none -> 5.27 us  [shards(): lax.all_to_all(product.reshape(ring, rows // ring, tiles * LANES), RING,...]
  transfers between devices with their start and end apart: 1 -> 3, of which waited for: 1 -> 2; matrix products, arithmetic and copies ran while one was open for 0% -> 0% of each run, Pallas kernels for 0% -> 0%
where the time goes in v1:
time: 276 us; the launch traced here: 274 us
  waiting for transfers between devices  118 us (43%)
  blocking collectives  87.1 us (32%)
  local copies, waits for them, and re-layouts  34.2 us (12%)
  between operations  14.2 us (5%)
  matrix products  8.67 us (3%)
  other arithmetic  7.27 us (3%)
  starting transfers between devices  5.32 us (2%)
    all_gather x1, waiting for transfers between devices, shards(): cols = lax.all_gather(own, PLANE, axis=0, tiled=True)  91.9 us
    psum x4, blocking collectives, shards(): total = lax.psum(total, axis)  75.6 us
    all_gather x1, waiting for transfers between devices, shards(): left = lax.all_gather(left, RING, axis=0)  25.8 us
    transpose x1, local copies, waits for them, and re-layouts, shards(): out = out.reshape(ring, rows // ring, tiles, LANES).transpose(1, 2, 0, 3)  12.1 us
    all_to_all x1, blocking collectives, shards(): lax.all_to_all(slots, (RING, 'exp'), split_axis=0, concat_axis=0, tiled=T...  11.4 us
    dot_general x1, matrix products, shards(): lax.dot_general(left, cols, (((0,), (0,)), ((), ())), preferred_element_t...  8.46 us
    reshape x1, local copies, waits for them, and re-layouts, shards(): return out.reshape(1, rows // ring, ff)  8.18 us
    reshape x1, local copies, waits for them, and re-layouts, shards(): out = out.reshape(ring, rows // ring, tiles, LANES).transpose(1, 2, 0, 3)  7.9 us
  transfers between devices with their start and end apart: 3, of which 2 were waited for; matrix products, arithmetic and copies ran while one was open for 0% of the time, Pallas kernels for 0%

profile of v1, /device:TPU:6, one launch (start us, length us, event | category | flops | bytes accessed | tf_op | source)
XLA Modules:
  0.0 274.4 jit_solution(9909398859649748255)
XLA Ops:
  6.5 0.0 copy-start
  6.5 0.0 all-gather.4.cloned.1.call-start
  6.5 0.7 compare_reduce_fusion
  7.3 0.2 reduce_window_sum.11
  7.5 0.1 copy-done
  7.6 0.2 convolution_convert_fusion
  7.8 0.1 reshape.81
  8.0 0.1 reshape.82
  8.1 0.1 copy.18
  8.3 11.4 %all_to_all.10 = bf16[8,4,3584]{2,1,0:T(4,128)(2,1)S(1)} all-to-all(bf16[8,4,3584]{2,1,0:T(4,128)(2,1)S(1)} %copy.18), channel_id=1, replica_groups=mesh['tok_0'=4,'tok_1'=8,'tok_2'=4,'exp'=2] {'tok_2','exp'}, dimensions={0} | all-to-all | bytes 458752 | tf_op jit(solution)/shard_map/all_to_all | solution.py:38
  19.7 0.7 reshape.83
  20.4 0.0 all-gather.4.cloned.1.call-update
  20.5 0.0 all-gather.6.cloned.1.call-start
  20.6 91.9 %all-gather.4.cloned.1.call-done = bf16[1024,3584]{1,0:T(8,128)(2,1)} async-done(((bf16[32,3584]{1,0:T(8,128)(2,1)}), bf16[1024,3584]{1,0:T(8,128)(2,1)}) %all-gather.4.cloned.1.call-update) | async-done | bytes 7340048 | tf_op jit(solution)/shard_map/all_gather | solution.py:45
  112.5 1.7 constant_dynamic-slice_fusion
  114.2 0.0 all-gather.6.cloned.1.call-update
  114.2 25.8 %all-gather.6.cloned.1.call-done = bf16[4096,128]{1,0:T(8,128)(2,1)} async-done(((bf16[1024,128]{1,0:T(8,128)(2,1)}), bf16[4096,128]{1,0:T(8,128)(2,1)}) %all-gather.6.cloned.1.call-update) | async-done | bytes 1048592 | tf_op jit(solution)/shard_map/all_gather | solution.py:52
  140.0 2.0 gather_fusion
  142.0 0.2 select_bitcast_fusion
  142.2 0.5 copy.19
  142.7 8.5 %fusion = f32[448,3584]{1,0:T(8,128)} fusion(bf16[1024,3584]{1,0:T(8,128)(2,1)} %all-gather.4.cloned.1.call-done, bf16[1024,512]{0,1:T(8,128)(2,1)S(1)} %bitcast.25, s32[]{:T(128)S(6)} %select_n.67), kind=kOutput, calls=%fused_computation.4 | convolution fusion | flops 3288334336 | bytes 14680068 | tf_op jit(solution)/shard_map/dot_general | solution.py:56
  151.2 5.3 %all-to-all-start.1 = ((f32[4,112,3584]{2,1,0:T(8,128)}), f32[4,112,3584]{2,1,0:T(8,128)}, u32[]{:S(2)}, u32[]{:S(2)}) async-start(f32[4,112,3584]{2,1,0:T(8,128)} %bitcast.23), calls=%async_computation.1 | async-start | bytes 12845056 | tf_op jit(solution)/shard_map/all_to_all | solution.py:59
  156.5 0.1 convert_reduce_fusion
  156.6 7.5 %psum.28 = f32[2]{0:T(128)S(1)} all-reduce(f32[2]{0:T(128)S(1)} %convert_element_type.14), channel_id=1, replica_groups=mesh['tok_0'=4,'tok_1'=8,'tok_2'=4,'exp'=2] {'tok_0'}, use_global_device_ids=true, to_apply=%region_3.4 | all-reduce | flops 2 | bytes 16 | tf_op jit(solution)/shard_map/psum | solution.py:42
  164.1 17.4 %psum.29 = f32[2]{0:T(128)S(1)} all-reduce(f32[2]{0:T(128)S(1)} %psum.28), channel_id=1, replica_groups=mesh['tok_0'=4,'tok_1'=8,'tok_2'=4,'exp'=2] {'tok_1'}, use_global_device_ids=true, to_apply=%region_4.5 | all-reduce | flops 2 | bytes 16 | tf_op jit(solution)/shard_map/psum | solution.py:42
  181.5 48.1 %psum.30 = f32[2]{0:T(128)S(1)} all-reduce(f32[2]{0:T(128)S(1)} %psum.29), channel_id=1, replica_groups=mesh['tok_0'=4,'tok_1'=8,'tok_2'=4,'exp'=2] {'tok_2'}, use_global_device_ids=true, to_apply=%region_5.6 | all-reduce | flops 2 | bytes 16 | tf_op jit(solution)/shard_map/psum | solution.py:42
  229.6 2.6 psum.31
  232.2 0.6 dynamic_slice.11
  233.4 0.0 all-to-all-done.1
  233.4 6.0 %broadcast_multiply_fusion = f32[4,112,3584]{2,1,0:T(8,128)} fusion(f32[4,112,3584]{2,1,0:T(8,128)} %all-to-all-done.1, f32[]{:T(128)} %bitcast.9), kind=kLoop, calls=%fused_computation.2 | loop fusion | flops 1605632 | bytes 12845060 | tf_op jit(solution)/shard_map/mul | solution.py:62
  239.4 7.9 %reshape.86 = f32[4,112,28,128]{3,2,1,0:T(8,128)} reshape(f32[4,112,3584]{2,1,0:T(8,128)} %broadcast_multiply_fusion) | data formatting | bytes 12845056 | tf_op jit(solution)/shard_map/reshape | solution.py:63
  247.3 12.1 %copy.20 = f32[112,28,4,128]{3,2,1,0:T(4,128)} copy(f32[112,28,4,128]{3,1,0,2:T(8,128)} %bitcast.22) | data formatting | bytes 12845056 | tf_op jit(solution)/shard_map/transpose | solution.py:63
  259.4 8.2 %reshape.87 = f32[1,112,14336]{2,1,0:T(8,128)} reshape(f32[112,28,4,128]{3,2,1,0:T(4,128)} %copy.20) | data formatting | bytes 12845056 | tf_op jit(solution)/shard_map/reshape | solution.py:64
  (7 shorter events, 0.1 us)
Async XLA Ops:
  6.5 1.0 copy-start
  6.5 106.0 %all-gather.4.cloned.1.call-start = ((), (), s32[]{:S(2)}) async-start(), calls=%async_computation.2 | async-start | bytes 7569408 | tf_op jit(solution)/shard_map/all_gather | solution.py:45
  20.5 119.6 %all-gather.6.cloned.1.call-start = ((), (), s32[]{:S(2)}) async-start(), calls=%async_computation.3 | async-start | bytes 1310720 | tf_op jit(solution)/shard_map/all_gather | solution.py:52
  151.2 82.2 %all-to-all-start.1 = ((f32[4,112,3584]{2,1,0:T(8,128)}), f32[4,112,3584]{2,1,0:T(8,128)}, u32[]{:S(2)}, u32[]{:S(2)}) async-start(f32[4,112,3584]{2,1,0:T(8,128)} %bitcast.23), calls=%async_computation.1 | async-start | bytes 12845056 | tf_op jit(solution)/shard_map/all_to_all | solution.py:59
Sparse Core Ops, SparseCore 0:
  20.6 91.8 all-gather.3
  114.3 25.6 all-gather.5

commit v2 on v0

v2 whole, which is shorter than its diff:
```python
import functools

import jax
import jax.numpy as jnp
from jax import lax
from jax.experimental import pallas as pl
from jax.experimental.pallas import tpu as pltpu
from jax.sharding import Mesh
from jax.sharding import PartitionSpec as P

CAP = 4
LANES = 128
AX, AZ, AY, AE = "tok_0", "tok_1", "tok_2", "exp"
TOK = (AX, AZ, AY)
TOK_EXP = (AX, AZ, AY, AE)
NX, NZ, NY, NE = 4, 8, 4, 2
TOP_CODE = 32767.0

CHUNKS = ((1, 2), (2, 3), (2, 3), (2, 3), (2, 3), (1, 2), (1, 1))
FIRST = (0, 0, 1, 1, 2, 2, 3)
SECOND_Z = (2, 3, 4, 5, 6, 7, 8)
SECOND_X = (4, 5, 6, 7, 8, 9, 10)


def place_tokens(activations, expert_ids, window_size):
    expert_labels = jnp.arange(window_size, dtype=jnp.int32)
    routed = jnp.any(expert_ids[:, :, None] == expert_labels[None, None, :], axis=1).astype(
        jnp.int32
    )
    ranking = jnp.cumsum(routed, axis=0) - 1
    slot_labels = jnp.arange(CAP, dtype=jnp.int32)
    placement = (routed.T[:, None, :] == 1) & (ranking.T[:, None, :] == slot_labels[None, :, None])
    placement_b = placement.astype(jnp.bfloat16)
    send_slots = jnp.einsum(
        "gct,tf->gcf", placement_b, activations, preferred_element_type=jnp.float32
    ).astype(jnp.bfloat16)
    marks = jnp.sum(placement.astype(jnp.float32), axis=2).astype(jnp.bfloat16)
    return send_slots, marks


def remote(src, dst, send, recv, **where):
    return pltpu.make_async_remote_copy(
        src_ref=src,
        dst_ref=dst,
        send_sem=send,
        recv_sem=recv,
        device_id=where,
        device_id_type=pl.DeviceIdType.MESH,
    )


def wrap(index, count):
    return lax.rem(index + count, count)


class Ring:
    def __init__(self, axis, count, view, extent, send, recv):
        self.axis, self.count, self.view, self.extent = axis, count, view, extent
        self.send, self.recv = send, recv
        self.me = lax.axis_index(axis)
        self.steps = count // 2

    def copy(self, step, way):
        sign = 1 if way == 0 else -1
        block = wrap(self.me - sign * (step - 1), self.count)
        half = self.extent // 2
        at, size = (way * half, half) if step == self.steps else (0, self.extent)
        ref = self.view(block, at, size)
        to = wrap(self.me + sign, self.count)
        return remote(ref, ref, self.send.at[way], self.recv.at[step - 1, way], **{self.axis: to})

    def run(self, step):
        for way in (0, 1):
            now = self.copy(step, way)
            if step > 1:
                before = self.copy(step - 1, way)
                before.wait_recv()
                before.wait_send()
            now.start()

    def finish(self):
        for way in (0, 1):
            self.copy(self.steps, way).wait()


def kernel(
    slots, codes, scales,
    arrived, own, left1, left4, left, gx, gz, prod, code, scale, cx, cz,
    s_y, r_y, s_c, r_c, s_l1, r_l1, s_l2, r_l2, s_l3, r_l3,
    s_xf, r_xf, s_zs, r_zs, s_zf, r_zf, s_xs, r_xs, s_o, r_o, l_o,
):
    x, z, y, e = (lax.axis_index(a) for a in (AX, AZ, AY, AE))
    rows = prod.shape[0] // NY
    slab = NY * NE * CAP
    marks_at = own.shape[1]

    pairs = [(dy, de) for dy in range(NY) for de in range(NE) if (dy, de) != (0, 0)]
    barrier = pltpu.get_barrier_semaphore()
    for d in range(1, NX):
        pl.semaphore_signal(barrier, inc=1, device_id={AX: wrap(x + d, NX)}, device_id_type=pl.DeviceIdType.MESH)
    for d in range(1, NZ):
        pl.semaphore_signal(barrier, inc=1, device_id={AZ: wrap(z + d, NZ)}, device_id_type=pl.DeviceIdType.MESH)
    for dy, de in pairs:
        pl.semaphore_signal(barrier, inc=1, device_id={AY: wrap(y + dy, NY), AE: wrap(e + de, NE)}, device_id_type=pl.DeviceIdType.MESH)
    pl.semaphore_wait(barrier, NX - 1 + NZ - 1 + len(pairs))

    me = y * NE + e
    fetch = []
    for i, (dy, de) in enumerate(pairs):
        ty, te = wrap(y + dy, NY), wrap(e + de, NE)
        c = remote(slots.at[ty * NE + te], arrived.at[me], s_y.at[i], r_y.at[i], **{AY: ty, AE: te})
        c.start()
        fetch.append(c)
    arrived[me] = slots[me]
    for c in fetch:
        c.wait()

    mine = jnp.concatenate(
        [arrived[i, :, :marks_at].astype(jnp.float32) for i in range(NY * NE)], axis=0
    ).astype(jnp.bfloat16)
    own[...] = mine
    at_x = pl.ds(pl.multiple_of(x * slab, slab), slab)
    tile = 0
    spans = []
    px = pz = 0
    for a, b in CHUNKS:
        gx[z, at_x, px * LANES:(px + a) * LANES] = own[:, tile * LANES:(tile + a) * LANES]
        gz[z, at_x, pz * LANES:(pz + b) * LANES] = own[:, (tile + a) * LANES:(tile + a + b) * LANES]
        spans.append((tile, a, b, px, pz))
        tile, px, pz = tile + a + b, px + a, pz + b
    left1[at_x, :] = own[:, pl.ds(pl.multiple_of(x * left1.shape[1], LANES), left1.shape[1])]
    marks = sum(
        jnp.sum(arrived[i, :, marks_at:].astype(jnp.float32), axis=0, keepdims=True)
        for i in range(NY * NE)
    )
    cx[x] = jnp.broadcast_to(marks, cx.shape[1:])

    def rows_of(block, at, size):
        return pl.ds(pl.multiple_of(block * slab + at, 8), size)

    rings = []
    for c, (_, a, b, px, pz) in enumerate(spans):
        on_x, on_z = pl.ds(px * LANES, a * LANES), pl.ds(pz * LANES, b * LANES)
        rings.append((
            Ring(AX, NX, lambda k, at, m, w=on_x: gx.at[z, rows_of(k, at, m), w], slab, s_xf.at[c], r_xf.at[c]),
            Ring(AZ, NZ, lambda k, at, m, w=on_x: gx.at[k, pl.ds(at, m), w], NX * slab, s_zs.at[c], r_zs.at[c]),
            Ring(AZ, NZ, lambda k, at, m, w=on_z: gz.at[k, rows_of(x, at, m), w], slab, s_zf.at[c], r_zf.at[c]),
            Ring(AX, NX, lambda k, at, m, w=on_z: gz.at[pl.ds(at, m), rows_of(k, 0, slab), w], NZ, s_xs.at[c], r_xs.at[c]),
        ))

    def left_step1():
        out = []
        for d in range(1, NX):
            to = wrap(x + d, NX)
            w = left1.shape[1]
            c = remote(
                own.at[:, pl.ds(pl.multiple_of(to * w, LANES), w)], left1.at[at_x, :],
                s_l1.at[d], r_l1.at[d], **{AX: to},
            )
            c.start()
            out.append(c)
            c = remote(cx.at[x], cx.at[x], s_c.at[d], r_c.at[d], **{AX: to})
            c.start()
            out.append(c)
        return out

    def local_tile(zz):
        return lax.div(lax.div(7 * zz, 2) - y + (NY - 1), NY)

    def left_step2():
        cz[z] = sum(cx[i] for i in range(NX))
        out = []
        for d in (1, 7, 2, 6, 3, 5, 4):
            to = wrap(z + d, NZ)
            c = remote(
                left1.at[:, pl.ds(pl.multiple_of(local_tile(to) * LANES, LANES), LANES)], left4.at[y, z],
                s_l2.at[d], r_l2.at[d], **{AZ: to},
            )
            c.start()
            n = remote(cz.at[z], cz.at[z], s_c.at[NX + d], r_c.at[NX + d], **{AZ: to})
            n.start()
            out.append((c, n))
        left4[y, z] = left1[:, pl.ds(pl.multiple_of(local_tile(z) * LANES, LANES), LANES)]
        return out

    def left_step3(d):
        piece = wrap(z - d, NZ)
        out = []
        for dy in range(1, NY):
            c = remote(left4.at[y, piece], left4.at[y, piece], s_l3.at[d, dy], r_l3.at[d, dy], **{AY: wrap(y + dy, NY)})
            c.start()
            out.append(c)
        return out

    low = lax.div(7 * z, 2)
    off = pl.multiple_of(lax.rem(z, 2) * (LANES // 2), LANES // 2)
    k_all = NZ * NX * slab

    def transpose_left():
        for p in range(NY):
            yp = lax.rem(low + p, NY)
            for s in range(NZ):
                left[p * LANES:(p + 1) * LANES, s * LANES:(s + 1) * LANES] = left4[yp, s].T

    ways_out = []

    def multiply(c):
        t, a, b, px, pz = spans[c]
        w = (a + b) * LANES
        right = jnp.concatenate(
            [gx[:, :, px * LANES:(px + a) * LANES].reshape(k_all, a * LANES),
             gz[:, :, pz * LANES:(pz + b) * LANES].reshape(k_all, b * LANES)], axis=1)
        prod[:, :w] = jnp.dot(left[pl.ds(off, NY * rows), :], right, preferred_element_type=jnp.float32)
        at = pl.ds(t * LANES, w)
        factor = 2.0 / jnp.sum(cz[:, 0:1, 0:1], axis=0)

        def encode(i, carry):
            d = lax.rem(i + 1, NY)
            to = lax.rem(y + d, NY)
            v = prod[pl.ds(pl.multiple_of(to * rows, 16), rows), :w]
            m = jnp.max(jnp.abs(v), axis=0, keepdims=True)
            r = jnp.where(m > 0.0, 1.0 / jnp.where(m > 0.0, m, 1.0), 0.0)
            u = (jnp.sqrt(jnp.abs(v) * r) * TOP_CODE + 0.5).astype(jnp.int32)
            code[to, :, at] = jnp.where(v < 0.0, -u, u).astype(jnp.int16)
            scale[to, :, at] = m * factor
            return carry

        lax.fori_loop(0, NY, encode, 0)
        for dy in (1, 3, 2):
            to = wrap(y + dy, NY)
            for k, (src, dst) in enumerate(((code, codes), (scale, scales))):
                cp = remote(src.at[to, :, at], dst.at[y, :, at], s_o.at[c, dy, k], r_o.at[c, dy, k], **{AY: to})
                cp.start()
                ways_out.append(cp)
        for k, (src, dst) in enumerate(((code, codes), (scale, scales))):
            cp = pltpu.make_async_copy(src.at[y, :, at], dst.at[y, :, at], l_o.at[c, k])
            cp.start()
            ways_out.append(cp)

    n = len(CHUNKS)
    last = max(SECOND_Z[-1] + NZ // 2, SECOND_X[-1] + NX // 2)
    done1 = done2 = None
    done3 = []
    ready = False
    for r in range(last + 1):
        for c in range(n):
            xf, zs, zf, xs = rings[c]
            for ring, start in ((zs, SECOND_Z[c]), (xs, SECOND_X[c]), (zf, FIRST[c]), (xf, FIRST[c])):
                step = r - start + 1
                if 1 <= step <= ring.steps:
                    if ring is zs and step == 1:
                        xf.finish()
                    if ring is xs and step == 1:
                        zf.finish()
                    ring.run(step)
                elif step == ring.steps + 1 and ring in (zs, xs):
                    ring.finish()
            if r == 0 and c == 0:
                done1 = left_step1()
        if r == 1:
            for cp in done1:
                cp.wait()
            done2 = left_step2()
            done3 += left_step3(0)
        if r in (2, 3):
            for i, d in enumerate((1, 7, 2, 6, 3, 5, 4)):
                if (r == 2) == (i < 4):
                    for cp in done2[i]:
                        cp.wait()
                    done3 += left_step3(d)
        for c in range(n):
            if r == max(SECOND_Z[c] + NZ // 2, SECOND_X[c] + NX // 2):
                if not ready:
                    for cp in done3:
                        cp.wait()
                    transpose_left()
                    ready = True
                multiply(c)
    for cp in ways_out:
        cp.wait()


def exchange(slots):
    n = len(CHUNKS)
    tiles = sum(a + b for a, b in CHUNKS)
    t_x, t_z = (sum(c[i] for c in CHUNKS) for i in (0, 1))
    slab = NY * NE * CAP
    wide = max(a + b for a, b in CHUNKS) * LANES
    rows = tiles * LANES // (NX * NZ)
    bf16, f32, i16 = jnp.bfloat16, jnp.float32, jnp.int16
    dma = pltpu.SemaphoreType.DMA
    hbm = pl.BlockSpec(memory_space=pltpu.HBM)
    return pl.pallas_call(
        kernel,
        out_shape=(
            jax.ShapeDtypeStruct((NY, rows, tiles * LANES), i16),
            jax.ShapeDtypeStruct((NY, 1, tiles * LANES), f32),
        ),
        in_specs=[pl.BlockSpec(memory_space=pltpu.VMEM)],
        out_specs=(hbm, hbm),
        scratch_shapes=[
            pltpu.VMEM((NY * NE, CAP, (tiles + 1) * LANES), bf16),
            pltpu.VMEM((slab, tiles * LANES), bf16),
            pltpu.VMEM((NX * slab, tiles * LANES // NX), bf16),
            pltpu.VMEM((NY, NZ, NX * slab, LANES), bf16),
            pltpu.VMEM((NY * LANES, NZ * NX * slab), bf16),
            pltpu.VMEM((NZ, NX * slab, t_x * LANES), bf16),
            pltpu.VMEM((NZ, NX * slab, t_z * LANES), bf16),
            pltpu.VMEM((NY * rows, wide), f32),
            pltpu.VMEM((NY, rows, tiles * LANES), i16),
            pltpu.VMEM((NY, 1, tiles * LANES), f32),
            pltpu.VMEM((NX, 8, LANES), f32),
            pltpu.VMEM((NZ, 8, LANES), f32),
            dma((NY * NE,)), dma((NY * NE,)),
            dma((NX + NZ,)), dma((NX + NZ,)),
            dma((NX,)), dma((NX,)),
            dma((NZ,)), dma((NZ,)),
            dma((NZ, NY)), dma((NZ, NY)),
            dma((n, 2)), dma((n, NX // 2, 2)),
            dma((n, 2)), dma((n, NZ // 2, 2)),
            dma((n, 2)), dma((n, NZ // 2, 2)),
            dma((n, 2)), dma((n, NX // 2, 2)),
            dma((n, NY, 2)), dma((n, NY, 2)), dma((n, 2)),
        ],
        compiler_params=pltpu.CompilerParams(
            collective_id=0, has_side_effects=True, vmem_limit_bytes=48 * 1024 * 1024
        ),
        name="exchange",
    )(slots)


def decode_kernel(codes, scales, out):
    for j in range(codes.shape[2] // LANES):
        at = slice(j * LANES, (j + 1) * LANES)
        for y in range(NY):
            u = codes[y, :, at].astype(jnp.int32).astype(jnp.float32) * (1.0 / TOP_CODE)
            to = (j * NY + y) * LANES
            out[0, :, to:to + LANES] = u * jnp.abs(u) * scales[y, :, at]


def decode(codes, scales):
    _, rows, width = codes.shape
    step = 4 * LANES
    return pl.pallas_call(
        decode_kernel,
        grid=(width // step,),
        in_specs=[
            pl.BlockSpec((NY, rows, step), lambda i: (0, 0, i)),
            pl.BlockSpec((NY, 1, step), lambda i: (0, 0, i)),
        ],
        out_specs=pl.BlockSpec((1, rows, step * NY), lambda i: (0, 0, i)),
        out_shape=jax.ShapeDtypeStruct((1, rows, width * NY), jnp.float32),
        name="decode",
    )(codes, scales)


def shards(activations, expert_ids):
    ff = activations.shape[1]
    tiles = ff // (NY * LANES)
    slots, marks = place_tokens(activations, expert_ids, NE)
    slots = slots.reshape(NE, CAP, tiles, NY, LANES).transpose(3, 0, 1, 2, 4)
    slots = slots.reshape(NY, NE, CAP, tiles * LANES)
    marks = jnp.broadcast_to(marks[None, :, :, None], (NY, NE, CAP, LANES))
    slots = jnp.concatenate([slots, marks], axis=3).reshape(NY * NE, CAP, (tiles + 1) * LANES)
    codes, scales = exchange(slots)
    return decode(codes, scales)


def solution(mesh):
    split = Mesh(mesh.devices.reshape(NX, NZ, NY, NE), TOK_EXP)
    return jax.shard_map(
        shards,
        mesh=split,
        in_specs=(P(TOK_EXP, None), P(TOK_EXP, None)),
        out_specs=P(AE, TOK, None),
        check_vma=False,
    )
```

time: 255 us -> 104 us (0.41)
  waiting for transfers between devices: 152 us -> 0 us
  Pallas kernels: 0 us -> 99.3 us
  blocking collectives: 67.5 us -> 0 us
  matrix products: 17.1 us -> 0.21 us
  between operations: 14.2 us -> 0.07 us
    all_gather x1 -> x0, waiting for transfers between devices: 152 us -> none  [shards(): lax.all_gather(own_cols, TOK, axis=1, tiled=True)]
    pallas_call x0 -> x2, Pallas kernels: none -> 99.3 us  [the longest x1 92.5 us: exchange(): pl.pallas_call(kernel, out_shape=(jax.ShapeDtypeStruct((NY, rows, tiles *...]
    psum x3 -> x0, blocking collectives: 35.3 us -> none  [one_axis_at_a_time(): value = lax.psum(value, axis)]
    all_to_all x2 -> x0, blocking collectives: 32.3 us -> none  [the longest x1 28.4 us: shards(): lax.all_to_all(received, TOK, split_axis=1, concat_axis=0, tiled=True)]
    dot_general x1 -> x0, matrix products: 16.9 us -> none  [shards(): lax.dot_general(own_cols, lax.all_gather(own_cols, TOK, axis=1, tiled=Tru...]
  transfers between devices with their start and end apart: 1 -> 0, of which waited for: 1 -> 0; matrix products, arithmetic and copies ran while one was open for 0% -> 0% of each run, Pallas kernels for 0% -> 0%
where the time goes in v2:
time: 104 us
  Pallas kernels  99.3 us (95%)
  local copies, waits for them, and re-layouts  2.81 us (3%)
  other arithmetic  1.15 us (1%)
    pallas_call x1, Pallas kernels, exchange(): pl.pallas_call(kernel, out_shape=(jax.ShapeDtypeStruct((NY, rows, tiles *...  92.5 us
    pallas_call x1, Pallas kernels, decode(): pl.pallas_call(decode_kernel, grid=(width // step,), in_specs=[pl.BlockSp...  6.82 us
    unnamed x6, local copies, waits for them, and re-layouts  2.28 us

profile of v2, /device:TPU:6, one launch (start us, length us, event | category | flops | bytes accessed | tf_op | source)
XLA Modules:
  0.0 103.6 jit_solution(762925148552955884)
XLA Ops:
  0.0 0.0 copy-start
  0.0 0.7 compare_reduce_fusion
  0.8 0.2 reduce_window_sum.11
  1.0 0.1 convert_reduce_fusion
  1.1 0.1 broadcast_in_dim.8
  1.1 0.0 copy-done
  1.1 0.2 convolution_convert_fusion
  1.4 0.1 reshape.16
  1.6 0.1 concatenate.6
  1.7 0.1 copy.9
  1.8 0.1 pad_maximum_fusion.slots
  2.0 92.5 %exchange.1 = (s16[4,112,3584]{2,1,0:T(8,128)(2,1)S(1)}, f32[4,1,3584]{2,1,0:T(1,128)S(1)}) custom-call(bf16[8,4,3712]{2,1,0:T(4,128)(2,1)S(1)} %pad_maximum_fusion.slots), custom_call_target="tpu_custom_call" | custom-call | tf_op jit(solution)/shard_map/exchange/pallas_call | solution.py:293
  94.4 0.0 copy-start.1
  94.5 1.7 %copy-done.1 = s16[4,112,3584]{2,1,0:T(8,128)(2,1)} copy-done((s16[4,112,3584]{2,1,0:T(8,128)(2,1)}, s16[4,112,3584]{2,1,0:T(8,128)(2,1)S(1)}, u32[]{:S(2)}) %copy-start.1) | copy-done | bytes 3211288
  96.1 0.0 copy-start.2
  96.1 0.6 copy-done.2
  96.7 6.8 %decode.1 = f32[1,112,14336]{2,1,0:T(8,128)} custom-call(s16[4,112,3584]{2,1,0:T(8,128)(2,1)} %copy-done.1, f32[4,1,3584]{2,1,0:T(1,128)} %copy-done.2), custom_call_target="tpu_custom_call" | custom-call | tf_op jit(solution)/shard_map/decode/pallas_call | solution.py:344
  (4 shorter events, 0.1 us)
Async XLA Ops:
  0.0 1.1 %copy-start = (bf16[12,14336]{1,0:T(8,128)(2,1)S(1)}, bf16[12,14336]{1,0:T(8,128)(2,1)}, u32[]{:S(2)}) copy-start(bf16[12,14336]{1,0:T(8,128)(2,1)} %param.2) | copy-start | bytes 1032196
  94.4 1.7 %copy-start.1 = (s16[4,112,3584]{2,1,0:T(8,128)(2,1)}, s16[4,112,3584]{2,1,0:T(8,128)(2,1)S(1)}, u32[]{:S(2)}) copy-start(s16[4,112,3584]{2,1,0:T(8,128)(2,1)S(1)} %get-tuple-element.7.codes) | copy-start | bytes 9633796
  96.1 0.6 copy-start.2

commit v3 on v2

v3 whole, which is shorter than its diff:
```python
import functools

import jax
import jax.numpy as jnp
from jax import lax
from jax.experimental import pallas as pl
from jax.experimental.pallas import tpu as pltpu
from jax.sharding import Mesh
from jax.sharding import PartitionSpec as P

CAP = 4
LANES = 128
AX, AZ, AY, AE = "tok_0", "tok_1", "tok_2", "exp"
TOK = (AX, AZ, AY)
TOK_EXP = (AX, AZ, AY, AE)
NX, NZ, NY, NE = 4, 8, 4, 2
TOP_CODE = 32767.0

CHUNKS = ((1, 1), (1, 2), (1, 4), (1, 1), (1, 3), (2, 2), (1, 2), (2, 3))
DIRECT = 1
ORDER = (
    ("qz", 1, 1), ("qz", 6, 1), ("qz", 2, 1), ("l1", 0, 1), ("px", 1, 1), ("px", 0, 1), ("px", 2, 1), ("px", 3, 1),
    ("px", 6, 1), ("px", 5, 1), ("px", 4, 1), ("px", 7, 1), ("qz", 0, 1), ("qz", 3, 1), ("qz", 7, 1), ("qz", 1, 2),
    ("qz", 6, 2), ("qz", 4, 1), ("qz", 2, 2), ("qz", 5, 1), ("qz", 3, 2), ("l2", 0, 4), ("l3", 0, 0), ("qz", 1, 3),
    ("l2", 0, 3), ("qx", 0, 1), ("qz", 2, 3), ("pz", 0, 1), ("qz", 1, 4), ("qz", 5, 2), ("qx", 0, 2), ("qz", 3, 3),
    ("pz", 2, 1), ("l3", 0, 4), ("pz", 1, 1), ("l2", 0, 1), ("qz", 2, 4), ("l3", 0, 3), ("pz", 0, 2), ("qx", 1, 1),
    ("qz", 4, 2), ("l2", 0, 2), ("pz", 1, 2), ("l3", 0, 1), ("qx", 2, 1), ("qz", 3, 4), ("pz", 2, 2), ("pz", 0, 3),
    ("pz", 3, 1), ("qx", 1, 2), ("pz", 6, 1), ("qz", 4, 3), ("l3", 0, 2), ("qx", 3, 1), ("pz", 1, 3), ("pz", 2, 3),
    ("pz", 0, 4), ("pz", 4, 1), ("pz", 5, 1), ("qz", 4, 4), ("pz", 1, 4), ("qx", 2, 2), ("pz", 2, 4), ("qz", 5, 3),
    ("pz", 3, 2), ("mm", 0, 1), ("pz", 4, 2), ("qz", 7, 2), ("qx", 3, 2), ("qx", 4, 1), ("qz", 6, 3), ("mm", 1, 1),
    ("qz", 5, 4), ("pz", 3, 3), ("pz", 5, 2), ("mm", 2, 1), ("qz", 7, 3), ("qz", 6, 4), ("pz", 4, 3), ("qx", 5, 1),
    ("pz", 3, 4), ("pz", 7, 1), ("pz", 5, 3), ("qx", 4, 2), ("qx", 6, 1), ("pz", 4, 4), ("mm", 3, 1), ("qz", 7, 4),
    ("pz", 6, 2), ("qx", 5, 2), ("pz", 7, 2), ("pz", 5, 4), ("mm", 4, 1), ("qx", 7, 1), ("pz", 6, 3), ("pz", 7, 3),
    ("qx", 6, 2), ("mm", 5, 1), ("pz", 6, 4), ("pz", 7, 4), ("qx", 7, 2), ("mm", 6, 1), ("mm", 7, 1),
)


def place_tokens(activations, expert_ids, window_size):
    expert_labels = jnp.arange(window_size, dtype=jnp.int32)
    routed = jnp.any(expert_ids[:, :, None] == expert_labels[None, None, :], axis=1).astype(
        jnp.int32
    )
    ranking = jnp.cumsum(routed, axis=0) - 1
    slot_labels = jnp.arange(CAP, dtype=jnp.int32)
    placement = (routed.T[:, None, :] == 1) & (ranking.T[:, None, :] == slot_labels[None, :, None])
    placement_b = placement.astype(jnp.bfloat16)
    send_slots = jnp.einsum(
        "gct,tf->gcf", placement_b, activations, preferred_element_type=jnp.float32
    ).astype(jnp.bfloat16)
    marks = jnp.sum(placement.astype(jnp.float32), axis=2).astype(jnp.bfloat16)
    return send_slots, marks


def remote(src, dst, send, recv, **where):
    return pltpu.make_async_remote_copy(
        src_ref=src,
        dst_ref=dst,
        send_sem=send,
        recv_sem=recv,
        device_id=where,
        device_id_type=pl.DeviceIdType.MESH,
    )


def wrap(index, count):
    return lax.rem(index + count, count)


class Ring:
    def __init__(self, axis, count, view, extent, send, recv):
        self.axis, self.count, self.view, self.extent = axis, count, view, extent
        self.send, self.recv = send, recv
        self.me = lax.axis_index(axis)
        self.steps = count // 2

    def copy(self, step, way):
        sign = 1 if way == 0 else -1
        block = wrap(self.me - sign * (step - 1), self.count)
        half = self.extent // 2
        at, size = (way * half, half) if step == self.steps else (0, self.extent)
        ref = self.view(block, at, size)
        to = wrap(self.me + sign, self.count)
        return remote(ref, ref, self.send.at[way], self.recv.at[step - 1, way], **{self.axis: to})

    def run(self, step):
        for way in (0, 1):
            now = self.copy(step, way)
            if step > 1:
                before = self.copy(step - 1, way)
                before.wait_recv()
                before.wait_send()
            now.start()

    def finish(self):
        for way in (0, 1):
            self.copy(self.steps, way).wait()


class Direct:
    def __init__(self, axis, count, view, extent, send, recv, others):
        self.axis, self.count, self.view, self.extent = axis, count, view, extent
        self.send, self.recv, self.others = send, recv, others
        self.me = lax.axis_index(axis)
        self.steps = 1

    def run(self, step):
        ref = self.view(self.me, 0, self.extent)
        for d in sorted(range(1, self.count), key=lambda d: min(d, self.count - d)):
            to = wrap(self.me + d, self.count)
            remote(ref, ref, self.send, self.recv, **{self.axis: to}).start()

    def finish(self):
        remote(self.others, self.others, self.send, self.recv, **{self.axis: wrap(self.me + 1, self.count)}).wait()


def kernel(
    slots, codes, scales,
    arrived, own, left1, left4, left, gx, gz, prod, code, scale, cx, cz,
    s_y, r_y, s_c, r_c, s_l1, r_l1, s_l2, r_l2, s_l3, r_l3,
    s_xf, r_xf, s_zs, r_zs, s_zf, r_zf, s_xs, r_xs, s_zd, r_zd, s_o, r_o,
):
    x, z, y, e = (lax.axis_index(a) for a in (AX, AZ, AY, AE))
    rows = prod.shape[0] // NY
    slab = NY * NE * CAP
    marks_at = own.shape[1]

    pairs = [(dy, de) for dy in range(NY) for de in range(NE) if (dy, de) != (0, 0)]
    barrier = pltpu.get_barrier_semaphore()
    for d in range(1, NX):
        pl.semaphore_signal(barrier, inc=1, device_id={AX: wrap(x + d, NX)}, device_id_type=pl.DeviceIdType.MESH)
    for d in range(1, NZ):
        pl.semaphore_signal(barrier, inc=1, device_id={AZ: wrap(z + d, NZ)}, device_id_type=pl.DeviceIdType.MESH)
    for dy, de in pairs:
        pl.semaphore_signal(barrier, inc=1, device_id={AY: wrap(y + dy, NY), AE: wrap(e + de, NE)}, device_id_type=pl.DeviceIdType.MESH)
    pl.semaphore_wait(barrier, NX - 1 + NZ - 1 + len(pairs))

    me = y * NE + e
    for dy, de in pairs:
        ty, te = wrap(y + dy, NY), wrap(e + de, NE)
        remote(slots.at[ty * NE + te], arrived.at[me], s_y, r_y, **{AY: ty, AE: te}).start()
    arrived[me] = slots[me]
    most = pl.ds(0, len(pairs))
    remote(slots.at[most], arrived.at[most], s_y, r_y, **{AE: wrap(e + 1, NE)}).wait()

    mine = jnp.concatenate(
        [arrived[i, :, :marks_at].astype(jnp.float32) for i in range(NY * NE)], axis=0
    ).astype(jnp.bfloat16)
    own[...] = mine
    at_x = pl.ds(pl.multiple_of(x * slab, slab), slab)
    tile = 0
    spans = []
    px = pz = 0
    for a, b in CHUNKS:
        gx[z, at_x, px * LANES:(px + a) * LANES] = own[:, tile * LANES:(tile + a) * LANES]
        gz[z, at_x, pz * LANES:(pz + b) * LANES] = own[:, (tile + a) * LANES:(tile + a + b) * LANES]
        spans.append((tile, a, b, px, pz))
        tile, px, pz = tile + a + b, px + a, pz + b
    left1[at_x, :] = own[:, pl.ds(pl.multiple_of(x * left1.shape[1], LANES), left1.shape[1])]
    marks = sum(
        jnp.sum(arrived[i, :, marks_at:].astype(jnp.float32), axis=0, keepdims=True)
        for i in range(NY * NE)
    )
    cx[x] = jnp.broadcast_to(marks, cx.shape[1:])

    def rows_of(block, at, size):
        return pl.ds(pl.multiple_of(block * slab + at, 8), size)

    rings = []
    for c, (_, a, b, px, pz) in enumerate(spans):
        on_x, on_z = pl.ds(px * LANES, a * LANES), pl.ds(pz * LANES, b * LANES)
        rings.append((
            Direct(AX, NX, lambda k, at, m, w=on_x: gx.at[z, rows_of(k, at, m), w], slab, s_xf.at[c], r_xf.at[c],
                   gx.at[z, pl.ds(0, (NX - 1) * slab), on_x]),
            Ring(AZ, NZ, lambda k, at, m, w=on_x: gx.at[k, pl.ds(at, m), w], NX * slab, s_zs.at[c], r_zs.at[c]),
            Direct(AZ, NZ, lambda k, at, m, w=on_z: gz.at[k, rows_of(x, at, m), w], slab, s_zd.at[c], r_zd.at[c],
                   gz.at[pl.ds(0, NZ - 1), at_x, on_z])
            if c < DIRECT else
            Ring(AZ, NZ, lambda k, at, m, w=on_z: gz.at[k, rows_of(x, at, m), w], slab, s_zf.at[c], r_zf.at[c]),
            Ring(AX, NX, lambda k, at, m, w=on_z: gz.at[pl.ds(at, m), rows_of(k, 0, slab), w], NZ, s_xs.at[c], r_xs.at[c]),
        ))

    def left_step1():
        w = left1.shape[1]
        for d in range(1, NX):
            to = wrap(x + d, NX)
            remote(
                own.at[:, pl.ds(pl.multiple_of(to * w, LANES), w)], left1.at[at_x, :], s_l1, r_l1, **{AX: to}
            ).start()
            remote(cx.at[x], cx.at[x], s_c.at[0], r_c.at[0], **{AX: to}).start()

    def left_wait1():
        w, k = left1.shape[1], (NX - 1) * slab
        to = wrap(x + 1, NX)
        remote(own.at[:, pl.ds(0, (NX - 1) * w)], left1.at[pl.ds(0, k), :], s_l1, r_l1, **{AX: to}).wait()
        rest = cx.at[pl.ds(0, NX - 1)]
        remote(rest, rest, s_c.at[0], r_c.at[0], **{AX: to}).wait()
        cz[z] = sum(cx[i] for i in range(NX))
        left4[y, z] = left1[:, pl.ds(pl.multiple_of(local_tile(z) * LANES, LANES), LANES)]

    def local_tile(zz):
        return lax.div(lax.div(7 * zz, 2) - y + (NY - 1), NY)

    def left_copy2(d):
        to = wrap(z + d, NZ)
        return remote(
            left1.at[:, pl.ds(pl.multiple_of(local_tile(to) * LANES, LANES), LANES)], left4.at[y, z],
            s_l2.at[d], r_l2.at[d], **{AZ: to},
        )

    def left_step2(d):
        left_copy2(d).start()
        remote(cz.at[z], cz.at[z], s_c.at[1], r_c.at[1], **{AZ: wrap(z + d, NZ)}).start()

    def left_step3(d):
        piece = left4.at[y, wrap(z - d, NZ)]
        for dy in range(1, NY):
            remote(piece, piece, s_l3.at[dy], r_l3.at[dy], **{AY: wrap(y + dy, NY)}).start()

    def left_wait3():
        rest = cz.at[pl.ds(0, NZ - 1)]
        remote(rest, rest, s_c.at[1], r_c.at[1], **{AZ: wrap(z + 1, NZ)}).wait()
        for dy in range(1, NY):
            remote(left4.at[y], left4.at[wrap(y - dy, NY)], s_l3.at[dy], r_l3.at[dy], **{AY: wrap(y + dy, NY)}).wait()

    low = lax.div(7 * z, 2)
    off = pl.multiple_of(lax.rem(z, 2) * (LANES // 2), LANES // 2)
    k_all = NZ * NX * slab

    def transpose_left():
        for p in range(NY):
            yp = lax.rem(low + p, NY)
            for s in range(NZ):
                left[p * LANES:(p + 1) * LANES, s * LANES:(s + 1) * LANES] = left4[yp, s].T


    def multiply(c):
        t, a, b, px, pz = spans[c]
        w = (a + b) * LANES
        right = jnp.concatenate(
            [gx[:, :, px * LANES:(px + a) * LANES].reshape(k_all, a * LANES),
             gz[:, :, pz * LANES:(pz + b) * LANES].reshape(k_all, b * LANES)], axis=1)
        prod[:, :w] = jnp.dot(left[pl.ds(off, NY * rows), :], right, preferred_element_type=jnp.float32)
        factor = 2.0 / jnp.sum(cz[:, 0:1, 0:1], axis=0)

        def encode(i, carry):
            to = lax.rem(y + i + 1, NY)
            v = prod[pl.ds(pl.multiple_of(to * rows, 16), rows), :w]
            m = jnp.max(jnp.abs(v), axis=0, keepdims=True)
            r = jnp.where(m > 0.0, 1.0 / jnp.where(m > 0.0, m, 1.0), 0.0)
            u = (jnp.sqrt(jnp.abs(v) * r) * TOP_CODE + 0.5).astype(jnp.int32)
            code[to, :, t * LANES:t * LANES + w] = jnp.where(v < 0.0, -u, u).astype(jnp.int16)
            m = m * factor
            for j in range(a + b):
                scale[to, t + j] = m[:, j * LANES:(j + 1) * LANES]
            return carry

        lax.fori_loop(0, NY, encode, 0)
        for dy in (1, 3, 2):
            to = wrap(y + dy, NY)
            for j in range(t, t + a + b):
                remote(
                    code.at[to, :, pl.ds(j * LANES, LANES)], codes.at[:, lanes_of(j * NY + y)],
                    s_o.at[c, 0], r_o.at[c, 0], **{AY: to},
                ).start()
            remote(scale.at[to, pl.ds(t, a + b)], scales.at[pl.ds(t, a + b), y], s_o.at[c, 1], r_o.at[c, 1], **{AY: to}).start()
        for j in range(t, t + a + b):
            codes[:, lanes_of(j * NY + y)] = code[y, :, j * LANES:(j + 1) * LANES]
            scales[j, y] = scale[y, j]

    def lanes_of(tile):
        return pl.ds(pl.multiple_of(tile * LANES, LANES), LANES)

    def receive(c):
        k = (NY - 1) * (spans[c][1] + spans[c][2])
        to = wrap(y + 1, NY)
        whole = codes.at[:, pl.ds(0, k * LANES)]
        remote(whole, whole, s_o.at[c, 0], r_o.at[c, 0], **{AY: to}).wait()
        sizes = scales.at[pl.ds(0, k), 0]
        remote(sizes, sizes, s_o.at[c, 1], r_o.at[c, 1], **{AY: to}).wait()

    waited = False
    for kind, c, d in ORDER:
        if kind in ("l2", "l3") and not waited:
            left_wait1()
            waited = True
        if kind == "l1":
            left_step1()
        elif kind == "l2":
            for way in sorted({d, NZ - d}):
                left_step2(way)
        elif kind == "l3":
            for way in sorted({d, (NZ - d) % NZ}):
                if d:
                    left_copy2(way).wait()
                left_step3(way)
        elif kind == "mm":
            rings[c][1].finish()
            rings[c][3].finish()
            if c == 0:
                left_wait3()
                transpose_left()
            multiply(c)
        else:
            k = ("px", "pz", "qz", "qx").index(kind)
            if d == 1 and k in (1, 3):
                rings[c][k - 1].finish()
            rings[c][k].run(d)
    for c in range(len(CHUNKS)):
        receive(c)


def exchange(slots):
    n = len(CHUNKS)
    tiles = sum(a + b for a, b in CHUNKS)
    t_x, t_z = (sum(c[i] for c in CHUNKS) for i in (0, 1))
    slab = NY * NE * CAP
    wide = max(a + b for a, b in CHUNKS) * LANES
    rows = tiles * LANES // (NX * NZ)
    bf16, f32, i16 = jnp.bfloat16, jnp.float32, jnp.int16
    dma = pltpu.SemaphoreType.DMA
    vmem = pl.BlockSpec(memory_space=pltpu.VMEM)
    return pl.pallas_call(
        kernel,
        out_shape=(
            jax.ShapeDtypeStruct((rows, tiles * NY * LANES), i16),
            jax.ShapeDtypeStruct((tiles, NY, 1, LANES), f32),
        ),
        in_specs=[vmem],
        out_specs=(vmem, vmem),
        scratch_shapes=[
            pltpu.VMEM((NY * NE, CAP, (tiles + 1) * LANES), bf16),
            pltpu.VMEM((slab, tiles * LANES), bf16),
            pltpu.VMEM((NX * slab, tiles * LANES // NX), bf16),
            pltpu.VMEM((NY, NZ, NX * slab, LANES), bf16),
            pltpu.VMEM((NY * LANES, NZ * NX * slab), bf16),
            pltpu.VMEM((NZ, NX * slab, t_x * LANES), bf16),
            pltpu.VMEM((NZ, NX * slab, t_z * LANES), bf16),
            pltpu.VMEM((NY * rows, wide), f32),
            pltpu.VMEM((NY, rows, tiles * LANES), i16),
            pltpu.VMEM((NY, tiles, 1, LANES), f32),
            pltpu.VMEM((NX, 8, LANES), f32),
            pltpu.VMEM((NZ, 8, LANES), f32),
            dma(()), dma(()),
            dma((2,)), dma((2,)),
            dma(()), dma(()),
            dma((NZ,)), dma((NZ,)),
            dma((NY,)), dma((NY,)),
            dma((n,)), dma((n,)),
            dma((n, 2)), dma((n, NZ // 2, 2)),
            dma((n, 2)), dma((n, NZ // 2, 2)),
            dma((n, 2)), dma((n, NX // 2, 2)),
            dma((max(DIRECT, 1),)), dma((max(DIRECT, 1),)),
            dma((n, 2)), dma((n, 2)),
        ],
        compiler_params=pltpu.CompilerParams(
            collective_id=0, has_side_effects=True, vmem_limit_bytes=48 * 1024 * 1024
        ),
        name="exchange",
    )(slots)


def shards(activations, expert_ids):
    ff = activations.shape[1]
    tiles = ff // (NY * LANES)
    slots, marks = place_tokens(activations, expert_ids, NE)
    slots = slots.reshape(NE, CAP, tiles, NY, LANES).transpose(3, 0, 1, 2, 4)
    slots = slots.reshape(NY, NE, CAP, tiles * LANES)
    marks = jnp.broadcast_to(marks[None, :, :, None], (NY, NE, CAP, LANES))
    slots = jnp.concatenate([slots, marks], axis=3).reshape(NY * NE, CAP, (tiles + 1) * LANES)
    codes, scales = exchange(slots)
    u = codes.astype(jnp.float32) * (1.0 / TOP_CODE)
    return (u * jnp.abs(u) * scales.reshape(1, ff))[None]


def solution(mesh):
    split = Mesh(mesh.devices.reshape(NX, NZ, NY, NE), TOK_EXP)
    return jax.shard_map(
        shards,
        mesh=split,
        in_specs=(P(TOK_EXP, None), P(TOK_EXP, None)),
        out_specs=P(AE, TOK, None),
        check_vma=False,
    )
```

time: 104 us -> 87.1 us (0.84)
  Pallas kernels: 99.3 us -> 80.6 us
  other arithmetic: 1.15 us -> 5.61 us
  local copies, waits for them, and re-layouts: 2.81 us -> 0.54 us
    pallas_call x2 -> x1, Pallas kernels: 99.3 us -> 80.6 us  [exchange(): pl.pallas_call(kernel, out_shape=(jax.ShapeDtypeStruct((rows, tiles * NY...]
    broadcast_in_dim x0 -> x1, other arithmetic: none -> 4.46 us  [shards(): return (u * jnp.abs(u) * scales.reshape(1, ff))[None]]
    unnamed x6 -> x2, local copies, waits for them, and re-layouts: 2.28 us -> 0.01 us
where the time goes in v3:
time: 87.1 us; the launch traced here: 87 us
  Pallas kernels  80.6 us (93%)
  other arithmetic  5.61 us (6%)
    pallas_call x1, Pallas kernels, exchange(): pl.pallas_call(kernel, out_shape=(jax.ShapeDtypeStruct((rows, tiles * NY...  80.6 us
    broadcast_in_dim x1, other arithmetic, shards(): return (u * jnp.abs(u) * scales.reshape(1, ff))[None]  4.46 us

profile of v3, /device:TPU:6, one launch (start us, length us, event | category | flops | bytes accessed | tf_op | source)
XLA Modules:
  0.0 87.0 jit_solution(2027899345935604455)
XLA Ops:
  0.0 0.0 copy-start
  0.0 0.7 compare_reduce_fusion
  0.8 0.2 reduce_window_sum.11
  1.0 0.1 convert_reduce_fusion
  1.1 0.1 broadcast_in_dim.20
  1.1 0.0 copy-done
  1.1 0.2 convolution_convert_fusion
  1.4 0.1 reshape.18
  1.6 0.1 concatenate.6
  1.7 0.1 copy.9
  1.8 0.1 pad_maximum_fusion.slots
  2.0 80.6 %exchange.1 = (s16[112,14336]{1,0:T(8,128)(2,1)S(1)}, f32[28,4,1,128]{3,2,1,0:T(1,128)S(1)}) custom-call(bf16[8,4,3712]{2,1,0:T(4,128)(2,1)S(1)} %pad_maximum_fusion.slots), custom_call_target="tpu_custom_call" | custom-call | tf_op jit(solution)/shard_map/exchange/pallas_call | solution.py:322
  82.6 4.5 %fusion.1 = f32[1,112,14336]{2,1,0:T(8,128)} fusion(s16[112,14336]{1,0:T(8,128)(2,1)S(1)} %get-tuple-element.7, f32[14336]{0:T(1024)S(1)} %bitcast.16), kind=kLoop, calls=%fused_computation.3 | loop fusion | flops 8028160 | bytes 9691136 | tf_op jit(solution)/shard_map/broadcast_in_dim | solution.py:372
  (4 shorter events, 0.1 us)
Async XLA Ops:
  0.0 1.1 %copy-start = (bf16[12,14336]{1,0:T(8,128)(2,1)S(1)}, bf16[12,14336]{1,0:T(8,128)(2,1)}, u32[]{:S(2)}) copy-start(bf16[12,14336]{1,0:T(8,128)(2,1)} %param.2) | copy-start | bytes 1032196

commit v4 on v3

--- a/solution.py
+++ b/solution.py
@@ -16,39 +16,50 @@
 NX, NZ, NY, NE = 4, 8, 4, 2
 TOP_CODE = 32767.0
 
-CHUNKS = ((1, 1), (1, 2), (1, 4), (1, 1), (1, 3), (2, 2), (1, 2), (2, 3))
+CHUNKS = ((1, 1), (1, 3), (1, 2), (1, 3), (1, 1), (2, 3), (3, 1), (2, 2))
 DIRECT = 1
 ORDER = (
-    ("qz", 1, 1), ("qz", 6, 1), ("qz", 2, 1), ("l1", 0, 1), ("px", 1, 1), ("px", 0, 1), ("px", 2, 1), ("px", 3, 1),
-    ("px", 6, 1), ("px", 5, 1), ("px", 4, 1), ("px", 7, 1), ("qz", 0, 1), ("qz", 3, 1), ("qz", 7, 1), ("qz", 1, 2),
-    ("qz", 6, 2), ("qz", 4, 1), ("qz", 2, 2), ("qz", 5, 1), ("qz", 3, 2), ("l2", 0, 4), ("l3", 0, 0), ("qz", 1, 3),
-    ("l2", 0, 3), ("qx", 0, 1), ("qz", 2, 3), ("pz", 0, 1), ("qz", 1, 4), ("qz", 5, 2), ("qx", 0, 2), ("qz", 3, 3),
-    ("pz", 2, 1), ("l3", 0, 4), ("pz", 1, 1), ("l2", 0, 1), ("qz", 2, 4), ("l3", 0, 3), ("pz", 0, 2), ("qx", 1, 1),
-    ("qz", 4, 2), ("l2", 0, 2), ("pz", 1, 2), ("l3", 0, 1), ("qx", 2, 1), ("qz", 3, 4), ("pz", 2, 2), ("pz", 0, 3),
-    ("pz", 3, 1), ("qx", 1, 2), ("pz", 6, 1), ("qz", 4, 3), ("l3", 0, 2), ("qx", 3, 1), ("pz", 1, 3), ("pz", 2, 3),
-    ("pz", 0, 4), ("pz", 4, 1), ("pz", 5, 1), ("qz", 4, 4), ("pz", 1, 4), ("qx", 2, 2), ("pz", 2, 4), ("qz", 5, 3),
-    ("pz", 3, 2), ("mm", 0, 1), ("pz", 4, 2), ("qz", 7, 2), ("qx", 3, 2), ("qx", 4, 1), ("qz", 6, 3), ("mm", 1, 1),
-    ("qz", 5, 4), ("pz", 3, 3), ("pz", 5, 2), ("mm", 2, 1), ("qz", 7, 3), ("qz", 6, 4), ("pz", 4, 3), ("qx", 5, 1),
-    ("pz", 3, 4), ("pz", 7, 1), ("pz", 5, 3), ("qx", 4, 2), ("qx", 6, 1), ("pz", 4, 4), ("mm", 3, 1), ("qz", 7, 4),
-    ("pz", 6, 2), ("qx", 5, 2), ("pz", 7, 2), ("pz", 5, 4), ("mm", 4, 1), ("qx", 7, 1), ("pz", 6, 3), ("pz", 7, 3),
-    ("qx", 6, 2), ("mm", 5, 1), ("pz", 6, 4), ("pz", 7, 4), ("qx", 7, 2), ("mm", 6, 1), ("mm", 7, 1),
+    ("l1", 0, 1), ("qz", 4, 1), ("px", 6, 1), ("qz", 7, 1), ("px", 7, 1), ("px", 5, 1), ("px", 0, 1), ("px", 4, 1),
+    ("px", 2, 1), ("px", 3, 1), ("qz", 1, 1), ("px", 1, 1), ("qz", 2, 1), ("qz", 6, 1), ("qz", 0, 1), ("qz", 4, 2),
+    ("qz", 7, 2), ("qz", 1, 2), ("qz", 6, 2), ("qz", 2, 2), ("qz", 5, 1), ("qz", 3, 1), ("l3", 0, 0), ("l2", 0, 1),
+    ("qz", 4, 3), ("qz", 1, 3), ("qz", 6, 3), ("l2", 0, 2), ("qx", 0, 1), ("qz", 3, 2), ("l3", 0, 1), ("qz", 4, 4),
+    ("pz", 0, 1), ("qz", 1, 4), ("qz", 2, 3), ("pz", 1, 1), ("l2", 0, 3), ("qx", 0, 2), ("qx", 4, 1), ("l3", 0, 2),
+    ("qx", 1, 1), ("qz", 2, 4), ("pz", 0, 2), ("l2", 0, 4), ("pz", 1, 2), ("qx", 4, 2), ("qx", 2, 1), ("qz", 3, 3),
+    ("pz", 0, 3), ("l3", 0, 3), ("pz", 2, 1), ("pz", 3, 1), ("pz", 1, 3), ("qz", 3, 4), ("qz", 5, 2), ("qx", 1, 2),
+    ("l3", 0, 4), ("pz", 0, 4), ("pz", 2, 2), ("pz", 3, 2), ("pz", 1, 4), ("qx", 3, 1), ("pz", 5, 1), ("qx", 2, 2),
+    ("qz", 5, 3), ("pz", 2, 3), ("mm", 0, 1), ("pz", 3, 3), ("mm", 0, 2), ("mm", 0, 3), ("pz", 4, 1), ("mm", 1, 1),
+    ("pz", 5, 2), ("mm", 1, 2), ("mm", 1, 3), ("pz", 2, 4), ("qz", 5, 4), ("pz", 3, 4), ("qz", 6, 4), ("pz", 4, 2),
+    ("qx", 3, 2), ("pz", 6, 1), ("mm", 2, 1), ("qx", 5, 1), ("qx", 6, 1), ("mm", 2, 2), ("pz", 5, 3), ("mm", 2, 3),
+    ("pz", 4, 3), ("mm", 3, 1), ("pz", 6, 2), ("mm", 3, 2), ("mm", 3, 3), ("pz", 5, 4), ("pz", 4, 4), ("qz", 7, 3),
+    ("pz", 7, 1), ("qx", 5, 2), ("pz", 6, 3), ("qx", 6, 2), ("mm", 4, 1), ("mm", 4, 2), ("mm", 4, 3), ("qz", 7, 4),
+    ("pz", 7, 2), ("mm", 5, 1), ("mm", 5, 2), ("pz", 6, 4), ("qx", 7, 1), ("mm", 5, 3), ("pz", 7, 3), ("mm", 6, 1),
+    ("mm", 6, 2), ("mm", 6, 3), ("qx", 7, 2), ("pz", 7, 4), ("mm", 7, 1), ("mm", 7, 2), ("mm", 7, 3),
 )
 
 
-def place_tokens(activations, expert_ids, window_size):
-    expert_labels = jnp.arange(window_size, dtype=jnp.int32)
-    routed = jnp.any(expert_ids[:, :, None] == expert_labels[None, None, :], axis=1).astype(
-        jnp.int32
-    )
-    ranking = jnp.cumsum(routed, axis=0) - 1
-    slot_labels = jnp.arange(CAP, dtype=jnp.int32)
-    placement = (routed.T[:, None, :] == 1) & (ranking.T[:, None, :] == slot_labels[None, :, None])
-    placement_b = placement.astype(jnp.bfloat16)
-    send_slots = jnp.einsum(
-        "gct,tf->gcf", placement_b, activations, preferred_element_type=jnp.float32
-    ).astype(jnp.bfloat16)
-    marks = jnp.sum(placement.astype(jnp.float32), axis=2).astype(jnp.bfloat16)
-    return send_slots, marks
+def place_tokens(acts, ids, slots, chosen):
+    named = ids[...]
+    n = named.shape[0]
+    row = lax.broadcasted_iota(jnp.int32, (n, n), 0)
+    column = lax.broadcasted_iota(jnp.int32, (n, n), 1)
+    slot = lax.broadcasted_iota(jnp.int32, (CAP, n), 0).astype(jnp.float32)
+    picks = []
+    for e in range(NE):
+        routed = jnp.max(jnp.where(named == e, 1.0, 0.0), axis=1, keepdims=True)
+        rank = jnp.sum(jnp.where(row < column, routed, 0.0), axis=0, keepdims=True)
+        here = jnp.sum(jnp.where(row == column, routed, 0.0), axis=0, keepdims=True)
+        picks.append(jnp.where((rank == slot) & (here > 0.0), 1.0, 0.0))
+    width = slots.shape[2] - LANES
+    pick = jnp.concatenate(picks, axis=0).astype(jnp.bfloat16)
+    chosen[...] = jnp.dot(pick, acts[...], preferred_element_type=jnp.float32)
+    for e in range(NE):
+        mark = jnp.broadcast_to(jnp.sum(picks[e], axis=1, keepdims=True), (CAP, LANES)).astype(jnp.bfloat16)
+        for y in range(NY):
+            slots[y * NE + e, :, :width] = jnp.concatenate(
+                [chosen[e * CAP:(e + 1) * CAP, (j * NY + y) * LANES:(j * NY + y + 1) * LANES] for j in range(width // LANES)],
+                axis=1,
+            ).astype(jnp.bfloat16)
+            slots[y * NE + e, :, width:] = mark
 
 
 def remote(src, dst, send, recv, **where):
@@ -67,33 +78,29 @@
 
 
 class Ring:
-    def __init__(self, axis, count, view, extent, send, recv):
+    def __init__(self, axis, count, view, extent, send, recv, two):
         self.axis, self.count, self.view, self.extent = axis, count, view, extent
-        self.send, self.recv = send, recv
+        self.send, self.recv, self.two = send, recv, two
         self.me = lax.axis_index(axis)
         self.steps = count // 2
 
-    def copy(self, step, way):
-        sign = 1 if way == 0 else -1
-        block = wrap(self.me - sign * (step - 1), self.count)
+    def wait(self, step):
+        ref = self.two if step < self.steps else self.view(self.me, 0, self.extent)
+        to = wrap(self.me + 1, self.count)
+        remote(ref, ref, self.send, self.recv.at[step - 1], **{self.axis: to}).wait()
+
+    def run(self, step):
+        if step > 1:
+            self.wait(step - 1)
         half = self.extent // 2
-        at, size = (way * half, half) if step == self.steps else (0, self.extent)
-        ref = self.view(block, at, size)
-        to = wrap(self.me + sign, self.count)
-        return remote(ref, ref, self.send.at[way], self.recv.at[step - 1, way], **{self.axis: to})
-
-    def run(self, step):
-        for way in (0, 1):
-            now = self.copy(step, way)
-            if step > 1:
-                before = self.copy(step - 1, way)
-                before.wait_recv()
-                before.wait_send()
-            now.start()
+        for way, sign in enumerate((1, -1)):
+            at, size = (way * half, half) if step == self.steps else (0, self.extent)
+            ref = self.view(wrap(self.me - sign * (step - 1), self.count), at, size)
+            to = wrap(self.me + sign, self.count)
+            remote(ref, ref, self.send, self.recv.at[step - 1], **{self.axis: to}).start()
 
     def finish(self):
-        for way in (0, 1):
-            self.copy(self.steps, way).wait()
+        self.wait(self.steps)
 
 
 class Direct:
@@ -114,8 +121,8 @@
 
 
 def kernel(
-    slots, codes, scales,
-    arrived, own, left1, left4, left, gx, gz, prod, code, scale, cx, cz,
+    acts, ids, codes, scales,
+    slots, chosen, arrived, own, left1, left4, left, gx, gz, prod, code, scale, cx, cz,
     s_y, r_y, s_c, r_c, s_l1, r_l1, s_l2, r_l2, s_l3, r_l3,
     s_xf, r_xf, s_zs, r_zs, s_zf, r_zf, s_xs, r_xs, s_zd, r_zd, s_o, r_o,
 ):
@@ -132,6 +139,7 @@
         pl.semaphore_signal(barrier, inc=1, device_id={AZ: wrap(z + d, NZ)}, device_id_type=pl.DeviceIdType.MESH)
     for dy, de in pairs:
         pl.semaphore_signal(barrier, inc=1, device_id={AY: wrap(y + dy, NY), AE: wrap(e + de, NE)}, device_id_type=pl.DeviceIdType.MESH)
+    place_tokens(acts, ids, slots, chosen)
     pl.semaphore_wait(barrier, NX - 1 + NZ - 1 + len(pairs))
 
     me = y * NE + e
@@ -171,12 +179,15 @@
         rings.append((
             Direct(AX, NX, lambda k, at, m, w=on_x: gx.at[z, rows_of(k, at, m), w], slab, s_xf.at[c], r_xf.at[c],
                    gx.at[z, pl.ds(0, (NX - 1) * slab), on_x]),
-            Ring(AZ, NZ, lambda k, at, m, w=on_x: gx.at[k, pl.ds(at, m), w], NX * slab, s_zs.at[c], r_zs.at[c]),
+            Ring(AZ, NZ, lambda k, at, m, w=on_x: gx.at[k, pl.ds(at, m), w], NX * slab, s_zs.at[c], r_zs.at[c],
+                 gx.at[pl.ds(0, 2), :, on_x]),
             Direct(AZ, NZ, lambda k, at, m, w=on_z: gz.at[k, rows_of(x, at, m), w], slab, s_zd.at[c], r_zd.at[c],
                    gz.at[pl.ds(0, NZ - 1), at_x, on_z])
             if c < DIRECT else
-            Ring(AZ, NZ, lambda k, at, m, w=on_z: gz.at[k, rows_of(x, at, m), w], slab, s_zf.at[c], r_zf.at[c]),
-            Ring(AX, NX, lambda k, at, m, w=on_z: gz.at[pl.ds(at, m), rows_of(k, 0, slab), w], NZ, s_xs.at[c], r_xs.at[c]),
+            Ring(AZ, NZ, lambda k, at, m, w=on_z: gz.at[k, rows_of(x, at, m), w], slab, s_zf.at[c], r_zf.at[c],
+                 gz.at[pl.ds(0, 2), at_x, on_z]),
+            Ring(AX, NX, lambda k, at, m, w=on_z: gz.at[pl.ds(at, m), rows_of(k, 0, slab), w], NZ, s_xs.at[c], r_xs.at[c],
+                 gz.at[:, pl.ds(0, 2 * slab), on_z]),
         ))
 
     def left_step1():
@@ -235,14 +246,27 @@
 
     def multiply(c):
         t, a, b, px, pz = spans[c]
-        w = (a + b) * LANES
         right = jnp.concatenate(
             [gx[:, :, px * LANES:(px + a) * LANES].reshape(k_all, a * LANES),
              gz[:, :, pz * LANES:(pz + b) * LANES].reshape(k_all, b * LANES)], axis=1)
-        prod[:, :w] = jnp.dot(left[pl.ds(off, NY * rows), :], right, preferred_element_type=jnp.float32)
+        prod[:, :(a + b) * LANES] = jnp.dot(
+            left[pl.ds(off, NY * rows), :], right, preferred_element_type=jnp.float32)
+
+    def send_out(c, to):
+        t, a, b, _, _ = spans[c]
+        for j in range(t, t + a + b):
+            remote(
+                code.at[to, :, pl.ds(j * LANES, LANES)], codes.at[:, lanes_of(j * NY + y)],
+                s_o.at[c, 0], r_o.at[c, 0], **{AY: to},
+            ).start()
+        remote(scale.at[to, pl.ds(t, a + b)], scales.at[pl.ds(t, a + b), y], s_o.at[c, 1], r_o.at[c, 1], **{AY: to}).start()
+
+    def encode(c, low, high):
+        t, a, b, _, _ = spans[c]
+        w = (a + b) * LANES
         factor = 2.0 / jnp.sum(cz[:, 0:1, 0:1], axis=0)
 
-        def encode(i, carry):
+        def one(i, carry):
             to = lax.rem(y + i + 1, NY)
             v = prod[pl.ds(pl.multiple_of(to * rows, 16), rows), :w]
             m = jnp.max(jnp.abs(v), axis=0, keepdims=True)
@@ -252,20 +276,18 @@
             m = m * factor
             for j in range(a + b):
                 scale[to, t + j] = m[:, j * LANES:(j + 1) * LANES]
+
+            @pl.when(i > 0)
+            def _():
+                send_out(c, lax.rem(y + i, NY))
+
             return carry
 
-        lax.fori_loop(0, NY, encode, 0)
-        for dy in (1, 3, 2):
-            to = wrap(y + dy, NY)
+        lax.fori_loop(low, high, one, 0)
+        if high == NY:
             for j in range(t, t + a + b):
-                remote(
-                    code.at[to, :, pl.ds(j * LANES, LANES)], codes.at[:, lanes_of(j * NY + y)],
-                    s_o.at[c, 0], r_o.at[c, 0], **{AY: to},
-                ).start()
-            remote(scale.at[to, pl.ds(t, a + b)], scales.at[pl.ds(t, a + b), y], s_o.at[c, 1], r_o.at[c, 1], **{AY: to}).start()
-        for j in range(t, t + a + b):
-            codes[:, lanes_of(j * NY + y)] = code[y, :, j * LANES:(j + 1) * LANES]
-            scales[j, y] = scale[y, j]
+                codes[:, lanes_of(j * NY + y)] = code[y, :, j * LANES:(j + 1) * LANES]
+                scales[j, y] = scale[y, j]
 
     def lanes_of(tile):
         return pl.ds(pl.multiple_of(tile * LANES, LANES), LANES)
@@ -294,12 +316,15 @@
                     left_copy2(way).wait()
                 left_step3(way)
         elif kind == "mm":
-            rings[c][1].finish()
-            rings[c][3].finish()
-            if c == 0:
-                left_wait3()
-                transpose_left()
-            multiply(c)
+            if d == 1:
+                rings[c][1].finish()
+                rings[c][3].finish()
+                if c == 0:
+                    left_wait3()
+                    transpose_left()
+                multiply(c)
+            else:
+                encode(c, *((0, NY // 2) if d == 2 else (NY // 2, NY)))
         else:
             k = ("px", "pz", "qz", "qx").index(kind)
             if d == 1 and k in (1, 3):
@@ -309,7 +334,7 @@
         receive(c)
 
 
-def exchange(slots):
+def exchange(acts, ids):
     n = len(CHUNKS)
     tiles = sum(a + b for a, b in CHUNKS)
     t_x, t_z = (sum(c[i] for c in CHUNKS) for i in (0, 1))
@@ -325,9 +350,11 @@
             jax.ShapeDtypeStruct((rows, tiles * NY * LANES), i16),
             jax.ShapeDtypeStruct((tiles, NY, 1, LANES), f32),
         ),
-        in_specs=[vmem],
+        in_specs=[vmem, vmem],
         out_specs=(vmem, vmem),
         scratch_shapes=[
+            pltpu.VMEM((NY * NE, CAP, (tiles + 1) * LANES), bf16),
+            pltpu.VMEM((NE * CAP, tiles * NY * LANES), f32),
             pltpu.VMEM((NY * NE, CAP, (tiles + 1) * LANES), bf16),
             pltpu.VMEM((slab, tiles * LANES), bf16),
             pltpu.VMEM((NX * slab, tiles * LANES // NX), bf16),
@@ -346,9 +373,9 @@
             dma((NZ,)), dma((NZ,)),
             dma((NY,)), dma((NY,)),
             dma((n,)), dma((n,)),
-            dma((n, 2)), dma((n, NZ // 2, 2)),
-            dma((n, 2)), dma((n, NZ // 2, 2)),
-            dma((n, 2)), dma((n, NX // 2, 2)),
+            dma((n,)), dma((n, NZ // 2)),
+            dma((n,)), dma((n, NZ // 2)),
+            dma((n,)), dma((n, NX // 2)),
             dma((max(DIRECT, 1),)), dma((max(DIRECT, 1),)),
             dma((n, 2)), dma((n, 2)),
         ],
@@ -356,18 +383,12 @@
             collective_id=0, has_side_effects=True, vmem_limit_bytes=48 * 1024 * 1024
         ),
         name="exchange",
-    )(slots)
+    )(acts, ids)
 
 
 def shards(activations, expert_ids):
     ff = activations.shape[1]
-    tiles = ff // (NY * LANES)
-    slots, marks = place_tokens(activations, expert_ids, NE)
-    slots = slots.reshape(NE, CAP, tiles, NY, LANES).transpose(3, 0, 1, 2, 4)
-    slots = slots.reshape(NY, NE, CAP, tiles * LANES)
-    marks = jnp.broadcast_to(marks[None, :, :, None], (NY, NE, CAP, LANES))
-    slots = jnp.concatenate([slots, marks], axis=3).reshape(NY * NE, CAP, (tiles + 1) * LANES)
-    codes, scales = exchange(slots)
+    codes, scales = exchange(activations, expert_ids)
     u = codes.astype(jnp.float32) * (1.0 / TOP_CODE)
     return (u * jnp.abs(u) * scales.reshape(1, ff))[None]
 

time: 87.1 us -> 85.1 us (0.977)
  Pallas kernels: 80.6 us -> 78.2 us
  local copies, waits for them, and re-layouts: 0.54 us -> 1.78 us
  other arithmetic: 5.61 us -> 4.46 us
    pallas_call x1, Pallas kernels: 80.6 us -> 78.2 us  [exchange(): pl.pallas_call(kernel, out_shape=(jax.ShapeDtypeStruct((rows, tiles * NY...]
    unnamed x2 -> x3, local copies, waits for them, and re-layouts: 0.01 us -> 1.78 us
where the time goes in v4:
time: 85.1 us; the launch traced here: 84.5 us
  Pallas kernels  78.2 us (92%)
  other arithmetic  4.46 us (5%)
  local copies, waits for them, and re-layouts  1.78 us (2%)
    pallas_call x1, Pallas kernels, exchange(): pl.pallas_call(kernel, out_shape=(jax.ShapeDtypeStruct((rows, tiles * NY...  78.2 us
    broadcast_in_dim x1, other arithmetic, shards(): return (u * jnp.abs(u) * scales.reshape(1, ff))[None]  4.46 us
    unnamed x3, local copies, waits for them, and re-layouts  1.78 us

profile of v4, /device:TPU:6, one launch (start us, length us, event | category | flops | bytes accessed | tf_op | source)
XLA Modules:
  0.0 84.5 jit_solution(8421448239210558085)
XLA Ops:
  0.0 0.8 copy.3.ids
  0.8 0.0 copy-start
  0.8 1.0 %copy-done = bf16[12,14336]{1,0:T(8,128)(2,1)S(1)} copy-done((bf16[12,14336]{1,0:T(8,128)(2,1)S(1)}, bf16[12,14336]{1,0:T(8,128)(2,1)}, u32[]{:S(2)}) %copy-start) | copy-done | bytes 344088
  1.8 78.2 %exchange.1 = (s16[112,14336]{1,0:T(8,128)(2,1)S(1)}, f32[28,4,1,128]{3,2,1,0:T(1,128)S(1)}) custom-call(bf16[12,14336]{1,0:T(8,128)(2,1)S(1)} %copy-done, s32[12,2]{1,0:T(8,128)S(1)} %copy.3.ids), custom_call_target="tpu_custom_call" | custom-call | tf_op jit(solution)/shard_map/exchange/pallas_call | solution.py:347
  80.0 4.5 %fusion.1 = f32[1,112,14336]{2,1,0:T(8,128)} fusion(s16[112,14336]{1,0:T(8,128)(2,1)S(1)} %get-tuple-element.7, f32[14336]{0:T(1024)S(1)} %bitcast.3), kind=kLoop, calls=%fused_computation.2 | loop fusion | flops 8028160 | bytes 9691136 | tf_op jit(solution)/shard_map/broadcast_in_dim | solution.py:393
Async XLA Ops:
  0.8 1.0 %copy-start = (bf16[12,14336]{1,0:T(8,128)(2,1)S(1)}, bf16[12,14336]{1,0:T(8,128)(2,1)}, u32[]{:S(2)}) copy-start(bf16[12,14336]{1,0:T(8,128)(2,1)} %acts.1) | copy-start | bytes 1032196

commit v5 on v4

--- a/solution.py
+++ b/solution.py
@@ -16,24 +16,24 @@
 NX, NZ, NY, NE = 4, 8, 4, 2
 TOP_CODE = 32767.0
 
-CHUNKS = ((1, 1), (1, 3), (1, 2), (1, 3), (1, 1), (2, 3), (3, 1), (2, 2))
+CHUNKS = ((1, 1), (1, 2), (1, 3), (2, 3), (1, 2), (1, 2), (1, 2), (4, 1))
 DIRECT = 1
 ORDER = (
-    ("l1", 0, 1), ("qz", 4, 1), ("px", 6, 1), ("qz", 7, 1), ("px", 7, 1), ("px", 5, 1), ("px", 0, 1), ("px", 4, 1),
-    ("px", 2, 1), ("px", 3, 1), ("qz", 1, 1), ("px", 1, 1), ("qz", 2, 1), ("qz", 6, 1), ("qz", 0, 1), ("qz", 4, 2),
-    ("qz", 7, 2), ("qz", 1, 2), ("qz", 6, 2), ("qz", 2, 2), ("qz", 5, 1), ("qz", 3, 1), ("l3", 0, 0), ("l2", 0, 1),
-    ("qz", 4, 3), ("qz", 1, 3), ("qz", 6, 3), ("l2", 0, 2), ("qx", 0, 1), ("qz", 3, 2), ("l3", 0, 1), ("qz", 4, 4),
-    ("pz", 0, 1), ("qz", 1, 4), ("qz", 2, 3), ("pz", 1, 1), ("l2", 0, 3), ("qx", 0, 2), ("qx", 4, 1), ("l3", 0, 2),
-    ("qx", 1, 1), ("qz", 2, 4), ("pz", 0, 2), ("l2", 0, 4), ("pz", 1, 2), ("qx", 4, 2), ("qx", 2, 1), ("qz", 3, 3),
-    ("pz", 0, 3), ("l3", 0, 3), ("pz", 2, 1), ("pz", 3, 1), ("pz", 1, 3), ("qz", 3, 4), ("qz", 5, 2), ("qx", 1, 2),
-    ("l3", 0, 4), ("pz", 0, 4), ("pz", 2, 2), ("pz", 3, 2), ("pz", 1, 4), ("qx", 3, 1), ("pz", 5, 1), ("qx", 2, 2),
-    ("qz", 5, 3), ("pz", 2, 3), ("mm", 0, 1), ("pz", 3, 3), ("mm", 0, 2), ("mm", 0, 3), ("pz", 4, 1), ("mm", 1, 1),
-    ("pz", 5, 2), ("mm", 1, 2), ("mm", 1, 3), ("pz", 2, 4), ("qz", 5, 4), ("pz", 3, 4), ("qz", 6, 4), ("pz", 4, 2),
-    ("qx", 3, 2), ("pz", 6, 1), ("mm", 2, 1), ("qx", 5, 1), ("qx", 6, 1), ("mm", 2, 2), ("pz", 5, 3), ("mm", 2, 3),
-    ("pz", 4, 3), ("mm", 3, 1), ("pz", 6, 2), ("mm", 3, 2), ("mm", 3, 3), ("pz", 5, 4), ("pz", 4, 4), ("qz", 7, 3),
-    ("pz", 7, 1), ("qx", 5, 2), ("pz", 6, 3), ("qx", 6, 2), ("mm", 4, 1), ("mm", 4, 2), ("mm", 4, 3), ("qz", 7, 4),
-    ("pz", 7, 2), ("mm", 5, 1), ("mm", 5, 2), ("pz", 6, 4), ("qx", 7, 1), ("mm", 5, 3), ("pz", 7, 3), ("mm", 6, 1),
-    ("mm", 6, 2), ("mm", 6, 3), ("qx", 7, 2), ("pz", 7, 4), ("mm", 7, 1), ("mm", 7, 2), ("mm", 7, 3),
+    ("px", 0, 1), ("px", 1, 1), ("px", 5, 1), ("l1", 0, 1), ("qz", 1, 1), ("qz", 2, 1), ("qz", 4, 1), ("qz", 0, 1),
+    ("px", 7, 1), ("qz", 3, 1), ("px", 2, 1), ("px", 4, 1), ("qz", 1, 2), ("px", 3, 1), ("pz", 0, 1), ("px", 6, 1),
+    ("pz", 1, 1), ("qz", 4, 2), ("qz", 2, 2), ("qz", 7, 1), ("qz", 3, 2), ("qz", 1, 3), ("l3", 0, 0), ("l2", 0, 2),
+    ("qx", 0, 1), ("l2", 0, 1), ("qz", 2, 3), ("l2", 0, 4), ("qz", 1, 4), ("pz", 0, 2), ("qx", 0, 2), ("l3", 0, 2),
+    ("l3", 0, 1), ("l2", 0, 3), ("qx", 1, 1), ("qz", 3, 3), ("qz", 2, 4), ("pz", 0, 3), ("pz", 1, 2), ("l3", 0, 4),
+    ("qz", 4, 3), ("pz", 2, 1), ("qz", 3, 4), ("qx", 2, 1), ("qz", 5, 1), ("qz", 6, 1), ("l3", 0, 3), ("pz", 0, 4),
+    ("pz", 3, 1), ("qx", 1, 2), ("pz", 1, 3), ("qz", 4, 4), ("qx", 3, 1), ("pz", 2, 2), ("pz", 4, 1), ("qz", 6, 2),
+    ("qz", 5, 2), ("pz", 3, 2), ("pz", 1, 4), ("mm", 0, 1), ("pz", 2, 3), ("qx", 2, 2), ("mm", 0, 2), ("qz", 5, 3),
+    ("mm", 0, 3), ("qz", 6, 3), ("pz", 5, 1), ("qx", 4, 1), ("pz", 3, 3), ("mm", 1, 1), ("mm", 1, 2), ("mm", 1, 3),
+    ("pz", 2, 4), ("qz", 5, 4), ("qz", 6, 4), ("qz", 7, 2), ("pz", 4, 2), ("qx", 3, 2), ("pz", 5, 2), ("pz", 6, 1),
+    ("pz", 3, 4), ("mm", 2, 1), ("qz", 7, 3), ("qx", 5, 1), ("mm", 2, 2), ("pz", 4, 3), ("mm", 2, 3), ("pz", 5, 3),
+    ("pz", 7, 1), ("qx", 4, 2), ("qx", 6, 1), ("mm", 3, 1), ("qz", 7, 4), ("pz", 5, 4), ("mm", 3, 2), ("pz", 4, 4),
+    ("mm", 3, 3), ("pz", 6, 2), ("qx", 5, 2), ("pz", 7, 2), ("qx", 7, 1), ("mm", 4, 1), ("mm", 4, 2), ("mm", 4, 3),
+    ("pz", 6, 3), ("qx", 6, 2), ("pz", 7, 3), ("mm", 5, 1), ("mm", 5, 2), ("mm", 5, 3), ("qx", 7, 2), ("pz", 6, 4),
+    ("pz", 7, 4), ("mm", 6, 1), ("mm", 6, 2), ("mm", 6, 3), ("mm", 7, 1), ("mm", 7, 2), ("mm", 7, 3),
 )
 
 

time: 85.1 us -> 85.6 us (level)
  Pallas kernels: 78.2 us -> 79.3 us
    pallas_call x1, Pallas kernels: 78.2 us -> 79.3 us  [exchange(): pl.pallas_call(kernel, out_shape=(jax.ShapeDtypeStruct((rows, tiles * NY...]
where the time goes in v5:
time: 85.6 us; the launch traced here: 85.5 us
  Pallas kernels  79.3 us (93%)
  other arithmetic  4.46 us (5%)
  local copies, waits for them, and re-layouts  1.78 us (2%)
    pallas_call x1, Pallas kernels, exchange(): pl.pallas_call(kernel, out_shape=(jax.ShapeDtypeStruct((rows, tiles * NY...  79.3 us
    broadcast_in_dim x1, other arithmetic, shards(): return (u * jnp.abs(u) * scales.reshape(1, ff))[None]  4.46 us
    unnamed x3, local copies, waits for them, and re-layouts  1.78 us

profile of v5, /device:TPU:6, one launch (start us, length us, event | category | flops | bytes accessed | tf_op | source)
XLA Modules:
  0.0 85.5 jit_solution(2243726264195989468)
XLA Ops:
  0.0 0.8 copy.3.ids
  0.8 0.0 copy-start
  0.8 1.0 %copy-done = bf16[12,14336]{1,0:T(8,128)(2,1)S(1)} copy-done((bf16[12,14336]{1,0:T(8,128)(2,1)S(1)}, bf16[12,14336]{1,0:T(8,128)(2,1)}, u32[]{:S(2)}) %copy-start) | copy-done | bytes 344088
  1.8 79.3 %exchange.1 = (s16[112,14336]{1,0:T(8,128)(2,1)S(1)}, f32[28,4,1,128]{3,2,1,0:T(1,128)S(1)}) custom-call(bf16[12,14336]{1,0:T(8,128)(2,1)S(1)} %copy-done, s32[12,2]{1,0:T(8,128)S(1)} %copy.3.ids), custom_call_target="tpu_custom_call" | custom-call | tf_op jit(solution)/shard_map/exchange/pallas_call | solution.py:347
  81.1 4.5 %fusion.1 = f32[1,112,14336]{2,1,0:T(8,128)} fusion(s16[112,14336]{1,0:T(8,128)(2,1)S(1)} %get-tuple-element.7, f32[14336]{0:T(1024)S(1)} %bitcast.3), kind=kLoop, calls=%fused_computation.2 | loop fusion | flops 8028160 | bytes 9691136 | tf_op jit(solution)/shard_map/broadcast_in_dim | solution.py:393
Async XLA Ops:
  0.8 1.0 %copy-start = (bf16[12,14336]{1,0:T(8,128)(2,1)S(1)}, bf16[12,14336]{1,0:T(8,128)(2,1)}, u32[]{:S(2)}) copy-start(bf16[12,14336]{1,0:T(8,128)(2,1)} %acts.1) | copy-start | bytes 1032196

commit v6 on v5

--- a/solution.py
+++ b/solution.py
@@ -16,24 +16,25 @@
 NX, NZ, NY, NE = 4, 8, 4, 2
 TOP_CODE = 32767.0
 
-CHUNKS = ((1, 1), (1, 2), (1, 3), (2, 3), (1, 2), (1, 2), (1, 2), (4, 1))
-DIRECT = 1
+CHUNKS = ((2, 2), (1, 2), (1, 1), (1, 2), (1, 2), (2, 2), (2, 2), (3, 2))
+DIRECT = 0
 ORDER = (
-    ("px", 0, 1), ("px", 1, 1), ("px", 5, 1), ("l1", 0, 1), ("qz", 1, 1), ("qz", 2, 1), ("qz", 4, 1), ("qz", 0, 1),
-    ("px", 7, 1), ("qz", 3, 1), ("px", 2, 1), ("px", 4, 1), ("qz", 1, 2), ("px", 3, 1), ("pz", 0, 1), ("px", 6, 1),
-    ("pz", 1, 1), ("qz", 4, 2), ("qz", 2, 2), ("qz", 7, 1), ("qz", 3, 2), ("qz", 1, 3), ("l3", 0, 0), ("l2", 0, 2),
-    ("qx", 0, 1), ("l2", 0, 1), ("qz", 2, 3), ("l2", 0, 4), ("qz", 1, 4), ("pz", 0, 2), ("qx", 0, 2), ("l3", 0, 2),
-    ("l3", 0, 1), ("l2", 0, 3), ("qx", 1, 1), ("qz", 3, 3), ("qz", 2, 4), ("pz", 0, 3), ("pz", 1, 2), ("l3", 0, 4),
-    ("qz", 4, 3), ("pz", 2, 1), ("qz", 3, 4), ("qx", 2, 1), ("qz", 5, 1), ("qz", 6, 1), ("l3", 0, 3), ("pz", 0, 4),
-    ("pz", 3, 1), ("qx", 1, 2), ("pz", 1, 3), ("qz", 4, 4), ("qx", 3, 1), ("pz", 2, 2), ("pz", 4, 1), ("qz", 6, 2),
-    ("qz", 5, 2), ("pz", 3, 2), ("pz", 1, 4), ("mm", 0, 1), ("pz", 2, 3), ("qx", 2, 2), ("mm", 0, 2), ("qz", 5, 3),
-    ("mm", 0, 3), ("qz", 6, 3), ("pz", 5, 1), ("qx", 4, 1), ("pz", 3, 3), ("mm", 1, 1), ("mm", 1, 2), ("mm", 1, 3),
-    ("pz", 2, 4), ("qz", 5, 4), ("qz", 6, 4), ("qz", 7, 2), ("pz", 4, 2), ("qx", 3, 2), ("pz", 5, 2), ("pz", 6, 1),
-    ("pz", 3, 4), ("mm", 2, 1), ("qz", 7, 3), ("qx", 5, 1), ("mm", 2, 2), ("pz", 4, 3), ("mm", 2, 3), ("pz", 5, 3),
-    ("pz", 7, 1), ("qx", 4, 2), ("qx", 6, 1), ("mm", 3, 1), ("qz", 7, 4), ("pz", 5, 4), ("mm", 3, 2), ("pz", 4, 4),
-    ("mm", 3, 3), ("pz", 6, 2), ("qx", 5, 2), ("pz", 7, 2), ("qx", 7, 1), ("mm", 4, 1), ("mm", 4, 2), ("mm", 4, 3),
-    ("pz", 6, 3), ("qx", 6, 2), ("pz", 7, 3), ("mm", 5, 1), ("mm", 5, 2), ("mm", 5, 3), ("qx", 7, 2), ("pz", 6, 4),
-    ("pz", 7, 4), ("mm", 6, 1), ("mm", 6, 2), ("mm", 6, 3), ("mm", 7, 1), ("mm", 7, 2), ("mm", 7, 3),
+    ("qz", 2, 1), ("l1", 0, 1), ("px", 5, 1), ("qz", 5, 1), ("px", 0, 1), ("px", 3, 1), ("qz", 0, 1), ("px", 1, 1),
+    ("px", 2, 1), ("px", 6, 1), ("qz", 3, 1), ("px", 7, 1), ("px", 4, 1), ("qz", 1, 1), ("qz", 7, 1), ("qz", 4, 1),
+    ("qz", 6, 1), ("qz", 2, 2), ("qz", 5, 2), ("qz", 0, 2), ("qz", 3, 2), ("qz", 1, 2), ("qz", 7, 2), ("qz", 4, 2),
+    ("qz", 6, 2), ("qz", 2, 3), ("l2", 0, 4), ("l3", 0, 0), ("qz", 0, 3), ("qz", 1, 3), ("l2", 0, 1), ("qz", 4, 3),
+    ("qz", 2, 4), ("pz", 0, 1), ("qz", 0, 4), ("l2", 0, 3), ("l3", 0, 1), ("qx", 2, 1), ("l3", 0, 4), ("qz", 1, 4),
+    ("pz", 4, 1), ("qx", 0, 1), ("pz", 0, 2), ("l2", 0, 2), ("qx", 2, 2), ("qx", 1, 1), ("qz", 4, 4), ("pz", 1, 1),
+    ("l3", 0, 3), ("qz", 3, 3), ("qz", 6, 3), ("pz", 0, 3), ("qx", 0, 2), ("qx", 4, 1), ("pz", 3, 1), ("l3", 0, 2),
+    ("pz", 1, 2), ("qz", 3, 4), ("qz", 6, 4), ("pz", 2, 1), ("pz", 4, 2), ("qx", 1, 2), ("pz", 0, 4), ("pz", 3, 2),
+    ("qx", 3, 1), ("qx", 6, 1), ("pz", 1, 3), ("pz", 2, 2), ("qz", 5, 3), ("pz", 5, 1), ("mm", 0, 1), ("mm", 0, 2),
+    ("pz", 1, 4), ("pz", 3, 3), ("mm", 0, 3), ("pz", 2, 3), ("qx", 4, 2), ("qz", 5, 4), ("pz", 4, 3), ("qz", 7, 3),
+    ("pz", 5, 2), ("mm", 1, 1), ("qx", 3, 2), ("mm", 1, 2), ("mm", 1, 3), ("pz", 2, 4), ("pz", 3, 4), ("qx", 5, 1),
+    ("pz", 6, 1), ("qx", 6, 2), ("pz", 4, 4), ("qz", 7, 4), ("pz", 7, 1), ("mm", 2, 1), ("mm", 2, 2), ("mm", 2, 3),
+    ("mm", 3, 1), ("pz", 5, 3), ("mm", 3, 2), ("qx", 7, 1), ("mm", 3, 3), ("pz", 6, 2), ("mm", 4, 1), ("mm", 4, 2),
+    ("mm", 4, 3), ("pz", 7, 2), ("qx", 5, 2), ("pz", 5, 4), ("pz", 6, 3), ("qx", 7, 2), ("pz", 7, 3), ("mm", 5, 1),
+    ("mm", 5, 2), ("mm", 5, 3), ("pz", 6, 4), ("pz", 7, 4), ("mm", 6, 1), ("mm", 6, 2), ("mm", 6, 3), ("mm", 7, 1),
+    ("mm", 7, 2), ("mm", 7, 3),
 )
 
 

time: 85.6 us -> 86.6 us (1.012)
  Pallas kernels: 79.3 us -> 80.2 us
    pallas_call x1, Pallas kernels: 79.3 us -> 80.2 us  [exchange(): pl.pallas_call(kernel, out_shape=(jax.ShapeDtypeStruct((rows, tiles * NY...]
where the time goes in v6:
time: 86.6 us; the launch traced here: 86.5 us
  Pallas kernels  80.2 us (93%)
  other arithmetic  4.46 us (5%)
  local copies, waits for them, and re-layouts  1.78 us (2%)
    pallas_call x1, Pallas kernels, exchange(): pl.pallas_call(kernel, out_shape=(jax.ShapeDtypeStruct((rows, tiles * NY...  80.2 us
    broadcast_in_dim x1, other arithmetic, shards(): return (u * jnp.abs(u) * scales.reshape(1, ff))[None]  4.46 us
    unnamed x3, local copies, waits for them, and re-layouts  1.78 us

profile of v6, /device:TPU:6, one launch (start us, length us, event | category | flops | bytes accessed | tf_op | source)
XLA Modules:
  0.0 86.5 jit_solution(7399039615088884411)
XLA Ops:
  0.0 0.8 copy.3.ids
  0.8 0.0 copy-start
  0.8 1.0 %copy-done = bf16[12,14336]{1,0:T(8,128)(2,1)S(1)} copy-done((bf16[12,14336]{1,0:T(8,128)(2,1)S(1)}, bf16[12,14336]{1,0:T(8,128)(2,1)}, u32[]{:S(2)}) %copy-start) | copy-done | bytes 344088
  1.8 80.2 %exchange.1 = (s16[112,14336]{1,0:T(8,128)(2,1)S(1)}, f32[28,4,1,128]{3,2,1,0:T(1,128)S(1)}) custom-call(bf16[12,14336]{1,0:T(8,128)(2,1)S(1)} %copy-done, s32[12,2]{1,0:T(8,128)S(1)} %copy.3.ids), custom_call_target="tpu_custom_call" | custom-call | tf_op jit(solution)/shard_map/exchange/pallas_call | solution.py:348
  82.0 4.5 %fusion.1 = f32[1,112,14336]{2,1,0:T(8,128)} fusion(s16[112,14336]{1,0:T(8,128)(2,1)S(1)} %get-tuple-element.7, f32[14336]{0:T(1024)S(1)} %bitcast.3), kind=kLoop, calls=%fused_computation.2 | loop fusion | flops 8028160 | bytes 9691136 | tf_op jit(solution)/shard_map/broadcast_in_dim | solution.py:394
Async XLA Ops:
  0.8 1.0 %copy-start = (bf16[12,14336]{1,0:T(8,128)(2,1)S(1)}, bf16[12,14336]{1,0:T(8,128)(2,1)}, u32[]{:S(2)}) copy-start(bf16[12,14336]{1,0:T(8,128)(2,1)} %acts.1) | copy-start | bytes 1032196
